TPU v7x, 512 devices: a whole 4x4x16 slice. The times are simulated.
512 devices in a mesh: tile: 128 (over y, z, core), lev: 4 (over x).
Axes of the slice: x: 4, y: 4, z: 16, core: 2. Of those that a mesh axis runs over, the one named last changes fastest.
Arguments:
- trajectory: bfloat16 [3, 32, 262144], P(None, 'lev', 'tile'), may hold values from -6 to 6
- increment: bfloat16 [3, 32, 262144], P(None, 'lev', 'tile'), may hold values from -6 to 6
- counts: int32 [128, 8], P('tile'), may hold values from 1 to 512, 2048 in all within a row
- remap_weight: bfloat16 [128, 8, 512, 512], P('tile'), may hold values from -0.25 to 0.25
- kappa: float32 [3], replicated, may hold values from 0.1 to 0.4
- courant: float32 [262144], P('tile'), may hold values from 0.1 to 0.6
- vertical: float32 [262144], P('tile'), may hold values from -0.4 to 0.4
- offset: int32 [262144], P('tile'), may hold values from -2 to 2
Outputs:
- tangent: float32 [3, 32, 262144], P(None, 'lev', 'tile')
- grad_outer: float32 [3, 32, 262144], P(None, 'lev', 'tile')
Inputs may be any that keep to these rules, and one draw needn't show every extreme that they name: Each row of counts sums to 2048, and every row has an entry equal to 512.
All inputs are finite; a program needn't handle non-finite values.
Results may differ from a plain program's by a relative error of at most 0.0021.
The roundings to bfloat16 on the way count: a program that leaves them out, or rounds other values in their place, can miss the bound.
Values may be sent and summed in bfloat16 or wider, within the bound.
A program may use at most 64 MiB of HBM per device.

v0:
```python
import jax
import jax.numpy as jnp
from jax import lax
from jax.sharding import PartitionSpec as P

HALO = 2


def from_behind(block, axis, distance):
    devices = range(lax.axis_size(axis))
    route = [((i - distance) % len(devices), i) for i in devices]
    return lax.ppermute(block, axis, route)


def padded(value, sides, width, wrap):
    for axis, dim in sides:
        size, length = (lax.axis_size(axis), value.shape[dim])
        up = [(i, (i + 1) % size) for i in range(size if wrap else size - 1)]
        down = [(j, i) for i, j in up]
        last = lax.slice_in_dim(value, length - width, length, axis=dim)
        leading = lax.slice_in_dim(value, 0, width, axis=dim)
        before = lax.ppermute(last, axis, up)
        after = lax.ppermute(leading, axis, down)
        value = jnp.concatenate([before, value, after], axis=dim)
    return value


def column_slots(sizes_row, slot_count, column_count):
    group_end = jnp.cumsum(sizes_row)
    group_start = group_end - sizes_row
    position = jnp.arange(slot_count, dtype=jnp.int32)
    slot_index = jnp.minimum(group_start[:, None] + position[None, :], column_count - 1)
    slot_live = position[None, :] < sizes_row[:, None]
    columns = jnp.arange(column_count, dtype=jnp.int32)
    owner = jnp.searchsorted(group_end, columns, side="right")
    back_index = owner * slot_count + columns - jnp.take(group_start, owner)
    return (slot_index, slot_live, back_index)


def forward_route(partial_value, reach_count, centre):
    pieces = []
    for which in range(reach_count):
        if which == centre:
            pieces.append(partial_value[which])
        else:
            pieces.append(from_behind(partial_value[which], "tile", which - centre))
    return jnp.stack(pieces)


def backward_route(windows, reach_count, centre):
    pieces = []
    for which in range(reach_count):
        if which == centre:
            pieces.append(windows[which])
        else:
            pieces.append(from_behind(windows[which], "tile", centre - which))
    return jnp.stack(pieces)


def shards(trajectory, increment, counts, remap_weight, kappa, courant, vertical, offset):
    tracers, level_count, outer_cols = trajectory.shape
    inner_cols = courant.shape[0]
    reach_count = remap_weight.shape[1]
    centre = reach_count // 2
    block_width = inner_cols // reach_count
    slot_count = remap_weight.shape[3]
    field_rows = tracers * level_count
    slot_index, slot_live, back_index = column_slots(counts[0], slot_count, outer_cols)
    fields = jnp.concatenate([trajectory, increment], axis=0).reshape(2 * field_rows, outer_cols)
    slotted = jnp.take(fields, slot_index.reshape(-1), axis=1).reshape(
        2 * field_rows, reach_count, slot_count
    )
    slotted = jnp.where(slot_live[None], slotted, jnp.zeros_like(slotted))
    weights = remap_weight[0]
    partial_value = jnp.einsum("fdc,dwc->dfw", slotted, weights, preferred_element_type=jnp.float32)
    received = forward_route(partial_value, reach_count, centre)
    blocks = received[:, :, :block_width] + jnp.roll(received[:, :, block_width:], 1, axis=0)
    remapped = jnp.transpose(blocks, (1, 0, 2)).reshape(2 * field_rows, inner_cols)
    state = remapped[:field_rows].reshape(tracers, level_count, inner_cols)
    delta = remapped[field_rows:].reshape(tracers, level_count, inner_cols)
    level_ext = padded(delta, (("lev", 1),), 1, False)
    side_ext = padded(delta, (("tile", 2),), HALO, True)
    rising = jnp.maximum(vertical, 0.0)
    sinking = jnp.maximum(-vertical, 0.0)
    departed = jnp.zeros_like(delta)
    for shift_by in range(-HALO, HALO + 1):
        moved_view = side_ext[:, :, HALO + shift_by : HALO + shift_by + inner_cols]
        departed = departed + jnp.where(offset == shift_by, moved_view, jnp.zeros_like(moved_view))
    below = level_ext[:, :-2]
    above = level_ext[:, 2:]
    loss = 2.0 * kappa[:, None, None] * state
    tangent = (
        delta
        + courant * (departed - delta)
        + rising * (below - delta)
        + sinking * (above - delta)
        - loss * delta
    )
    weight_rows = jnp.stack(
        [
            jnp.where(offset == shift_by, courant, jnp.zeros_like(courant))
            for shift_by in range(-HALO, HALO + 1)
        ]
    )
    joined = jnp.concatenate([tangent.reshape(field_rows, inner_cols), weight_rows], axis=0)
    joined_ext = padded(joined, (("tile", 1),), HALO, True)
    tangent_ext = padded(tangent, (("lev", 1),), 1, False)
    arrived_sum = jnp.zeros((field_rows, inner_cols), jnp.float32)
    for row_pos, shift_by in enumerate(range(-HALO, HALO + 1)):
        begin = HALO - shift_by
        view = joined_ext[:, begin : begin + inner_cols]
        arrived_sum = arrived_sum + view[field_rows + row_pos][None, :] * view[:field_rows]
    diagonal = 1.0 - courant - rising - sinking - loss
    adjoint = (
        diagonal * tangent
        + arrived_sum.reshape(tracers, level_count, inner_cols)
        + rising * tangent_ext[:, 2:]
        + sinking * tangent_ext[:, :-2]
    )
    adjoint_blocks = jnp.transpose(
        adjoint.reshape(field_rows, reach_count, block_width), (1, 0, 2)
    ).astype(jnp.bfloat16)
    windows = jnp.concatenate([adjoint_blocks, jnp.roll(adjoint_blocks, -1, axis=0)], axis=2)
    returned = backward_route(windows, reach_count, centre)
    slot_grad = jnp.einsum("dfw,dwc->fdc", returned, weights, preferred_element_type=jnp.float32)
    grad_outer = jnp.take(slot_grad.reshape(field_rows, -1), back_index, axis=1)
    return (tangent, grad_outer.reshape(tracers, level_count, outer_cols))


def solution(mesh):
    return jax.shard_map(
        shards,
        mesh=mesh,
        in_specs=(
            P(None, "lev", "tile"),
            P(None, "lev", "tile"),
            P("tile", None),
            P("tile", None, None, None),
            P(),
            P("tile"),
            P("tile"),
            P("tile"),
        ),
        out_specs=(P(None, "lev", "tile"), P(None, "lev", "tile")),
        check_vma=False,
    )
```

profile of v0, /device:TPU:1, one launch (start us, length us, event | category | flops | bytes accessed | tf_op | source)
XLA Modules:
  0.0 155.2 jit_solution(3707618196175830730)
XLA Ops:
  0.6 0.8 reduce-window.7
  2.2 0.7 iota_compare_fusion.1
  3.0 1.0 maximum_bitcast_fusion
  4.2 12.1 %gather_fusion = bf16[4096,48]{1,0:T(8,128)(2,1)S(1)} fusion(bf16[48,2048]{0,1:T(8,128)(2,1)S(1)} %copy.13, s32[4096]{0:T(1024)S(1)} %broadcast_clamp_fusion), kind=kCustom, calls=%fused_computation | custom fusion | bytes 802816 | tf_op jit(solution)/shard_map/jit(_take)/gather | solution.py:70
  16.8 3.5 %fusion.6 = f32[8,48,512]{2,1,0:T(8,128)S(1)} fusion(bf16[1,8,512,512]{3,2,1,0:T(8,128)(2,1)} %param.13, bf16[48,8,512]{2,0,1:T(8,128)(2,1)S(1)} %copy.14, pred[8,512]{1,0:T(8,128)(4,1)S(1)} %get-tuple-element.190, pred[8,512]{1,0:T(8,128)(4,1)S(1)} %get-tuple-element.189), kind=kOutput, calls=%fused_computation.9 | convolution fusion | flops 201719808 | bytes 5382144 | tf_op jit(solution)/shard_map/fdc,dwc->dfw/dot_general | solution.py:75
  20.3 14.8 %collective-permute-start = (f32[48,512]{1,0:T(8,128)S(1)}, f32[48,512]{1,0:T(8,128)S(1)}, u32[]{:S(2)}, u32[]{:S(2)}) collective-permute-start(f32[48,512]{1,0:T(8,128)S(1)} %get-tuple-element.123), channel_id=1, source_target_pairs={{16,0},{20,4},{24,8},{28,12},{32,16},{36,20},{40,24},{44,28},{48,3... | collective-permute-start | bytes 294920 | tf_op jit(solution)/shard_map/ppermute | solution.py:12
  35.2 3.5 %collective-permute-start.1 = (f32[48,512]{1,0:T(8,128)S(1)}, f32[48,512]{1,0:T(8,128)S(1)}, u32[]{:S(2)}, u32[]{:S(2)}) collective-permute-start(f32[48,512]{1,0:T(8,128)S(1)} %get-tuple-element.122), channel_id=1, source_target_pairs={{12,0},{16,4},{20,8},{24,12},{28,16},{32,20},{36,24},{40,28},{44,3... | collective-permute-start | bytes 294920 | tf_op jit(solution)/shard_map/ppermute | solution.py:12
  38.7 2.6 %collective-permute-start.2 = (f32[48,512]{1,0:T(8,128)S(1)}, f32[48,512]{1,0:T(8,128)S(1)}, u32[]{:S(2)}, u32[]{:S(2)}) collective-permute-start(f32[48,512]{1,0:T(8,128)S(1)} %get-tuple-element.121), channel_id=1, source_target_pairs={{8,0},{12,4},{16,8},{20,12},{24,16},{28,20},{32,24},{36,28},{40,32... | collective-permute-start | bytes 294920 | tf_op jit(solution)/shard_map/ppermute | solution.py:12
  41.3 3.4 %collective-permute-start.3 = (f32[48,512]{1,0:T(8,128)S(1)}, f32[48,512]{1,0:T(8,128)S(1)}, u32[]{:S(2)}, u32[]{:S(2)}) collective-permute-start(f32[48,512]{1,0:T(8,128)S(1)} %get-tuple-element.120), channel_id=1, source_target_pairs={{4,0},{8,4},{12,8},{16,12},{20,16},{24,20},{28,24},{32,28},{36,32}... | collective-permute-start | bytes 294920 | tf_op jit(solution)/shard_map/ppermute | solution.py:12
  44.7 22.4 %while.24 = (s32[]{:T(128)}, u32[2048]{0:T(1024)S(1)}, u32[2048]{0:T(1024)S(1)}, s32[8]{0:T(128)S(1)}, s32[]{:T(128)}, /*index=5*/s32[]{:T(128)}) while((s32[]{:T(128)}, u32[2048]{0:T(1024)S(1)}, u32[2048]{0:T(1024)S(1)}, s32[8]{0:T(128)S(1)}, s32[]{:T(128)}, /*index=5*/s32[]{:T(128)}) %tuple.111), condition=%wide.region_2.3_spmd.clone, body=%wide.region_1.2_spmd.clone.sunk | while | flops 45059 | bytes 32943 | solution.py:35
  44.7 0.7 fusion.74
  45.4 4.9 %fusion.75 = (u32[2048]{0:T(1024)S(1)}, u32[2048]{0:T(1024)S(1)}) fusion(u32[2048]{0:T(1024)S(1)} %get-tuple-element.244, u32[2048]{0:T(1024)S(1)} %get-tuple-element.243, s32[]{:T(128)} %bitcast.145, s32[]{:T(128)} %bitcast.146, s32[]{:T(128)} %bitcast.147, s32[]{:T(128)} %bitcast.148, s32[]{:T(128)} %bitcast.149, s32[]{:T(128)} %bitcast.150, ...), kind=kLoop, calls=%fused_computation.4.clone.1 | loop fusion | flops 45056 | bytes 32801 | tf_op jit(solution)/shard_map/jit(searchsorted)/jit(_searchsorted_scan_impl)/vmap(jit(_searchsorted_scan_impl))/while/body/eval_jaxpr/select_n | solution.py:35
  50.3 0.7 fusion.74
  51.0 4.9 %fusion.75 = (u32[2048]{0:T(1024)S(1)}, u32[2048]{0:T(1024)S(1)}) fusion(u32[2048]{0:T(1024)S(1)} %get-tuple-element.244, u32[2048]{0:T(1024)S(1)} %get-tuple-element.243, s32[]{:T(128)} %bitcast.145, s32[]{:T(128)} %bitcast.146, s32[]{:T(128)} %bitcast.147, s32[]{:T(128)} %bitcast.148, s32[]{:T(128)} %bitcast.149, s32[]{:T(128)} %bitcast.150, ...), kind=kLoop, calls=%fused_computation.4.clone.1 | loop fusion | flops 45056 | bytes 32801 | tf_op jit(solution)/shard_map/jit(searchsorted)/jit(_searchsorted_scan_impl)/vmap(jit(_searchsorted_scan_impl))/while/body/eval_jaxpr/select_n | solution.py:35
  55.9 0.7 fusion.74
  56.6 4.9 %fusion.75 = (u32[2048]{0:T(1024)S(1)}, u32[2048]{0:T(1024)S(1)}) fusion(u32[2048]{0:T(1024)S(1)} %get-tuple-element.244, u32[2048]{0:T(1024)S(1)} %get-tuple-element.243, s32[]{:T(128)} %bitcast.145, s32[]{:T(128)} %bitcast.146, s32[]{:T(128)} %bitcast.147, s32[]{:T(128)} %bitcast.148, s32[]{:T(128)} %bitcast.149, s32[]{:T(128)} %bitcast.150, ...), kind=kLoop, calls=%fused_computation.4.clone.1 | loop fusion | flops 45056 | bytes 32801 | tf_op jit(solution)/shard_map/jit(searchsorted)/jit(_searchsorted_scan_impl)/vmap(jit(_searchsorted_scan_impl))/while/body/eval_jaxpr/select_n | solution.py:35
  61.5 0.7 fusion.74
  62.2 4.9 %fusion.75 = (u32[2048]{0:T(1024)S(1)}, u32[2048]{0:T(1024)S(1)}) fusion(u32[2048]{0:T(1024)S(1)} %get-tuple-element.244, u32[2048]{0:T(1024)S(1)} %get-tuple-element.243, s32[]{:T(128)} %bitcast.145, s32[]{:T(128)} %bitcast.146, s32[]{:T(128)} %bitcast.147, s32[]{:T(128)} %bitcast.148, s32[]{:T(128)} %bitcast.149, s32[]{:T(128)} %bitcast.150, ...), kind=kLoop, calls=%fused_computation.4.clone.1 | loop fusion | flops 45056 | bytes 32801 | tf_op jit(solution)/shard_map/jit(searchsorted)/jit(_searchsorted_scan_impl)/vmap(jit(_searchsorted_scan_impl))/while/body/eval_jaxpr/select_n | solution.py:35
  67.3 2.2 %collective-permute-start.4 = (f32[48,512]{1,0:T(8,128)S(1)}, f32[48,512]{1,0:T(8,128)S(1)}, u32[]{:S(2)}, u32[]{:S(2)}) collective-permute-start(f32[48,512]{1,0:T(8,128)S(1)} %get-tuple-element.118), channel_id=1, source_target_pairs={{508,0},{0,4},{4,8},{8,12},{12,16},{16,20},{20,24},{24,28},{28,32}... | collective-permute-start | bytes 294920 | tf_op jit(solution)/shard_map/ppermute | solution.py:12
  69.5 0.7 fusion.70
  70.2 2.6 %collective-permute-start.5 = (f32[48,512]{1,0:T(8,128)S(1)}, f32[48,512]{1,0:T(8,128)S(1)}, u32[]{:S(2)}, u32[]{:S(2)}) collective-permute-start(f32[48,512]{1,0:T(8,128)S(1)} %get-tuple-element.117), channel_id=1, source_target_pairs={{504,0},{508,4},{0,8},{4,12},{8,16},{12,20},{16,24},{20,28},{24,32... | collective-permute-start | bytes 294920 | tf_op jit(solution)/shard_map/ppermute | solution.py:12
  72.8 2.7 %collective-permute-start.6 = (f32[48,512]{1,0:T(8,128)S(1)}, f32[48,512]{1,0:T(8,128)S(1)}, u32[]{:S(2)}, u32[]{:S(2)}) collective-permute-start(f32[48,512]{1,0:T(8,128)S(1)} %get-tuple-element.116), channel_id=1, source_target_pairs={{500,0},{504,4},{508,8},{0,12},{4,16},{8,20},{12,24},{16,28},{20,3... | collective-permute-start | bytes 294920 | tf_op jit(solution)/shard_map/ppermute | solution.py:12
  75.5 4.6 %collective-permute-done.5 = f32[48,512]{1,0:T(8,128)S(1)} collective-permute-done((f32[48,512]{1,0:T(8,128)S(1)}, f32[48,512]{1,0:T(8,128)S(1)}, u32[]{:S(2)}, u32[]{:S(2)}) %collective-permute-start.5) | collective-permute-done | bytes 98336 | tf_op jit(solution)/shard_map/ppermute | solution.py:12
  80.2 3.7 %collective-permute-done.6 = f32[48,512]{1,0:T(8,128)S(1)} collective-permute-done((f32[48,512]{1,0:T(8,128)S(1)}, f32[48,512]{1,0:T(8,128)S(1)}, u32[]{:S(2)}, u32[]{:S(2)}) %collective-permute-start.6) | collective-permute-done | bytes 98336 | tf_op jit(solution)/shard_map/ppermute | solution.py:12
  84.2 2.6 %collective-permute-start.8 = (f32[3,8,2]{2,1,0:T(8,128)S(1)}, f32[3,8,2]{2,1,0:T(8,128)S(1)}, u32[]{:S(2)}, u32[]{:S(2)}) collective-permute-start(f32[3,8,2]{2,1,0:T(8,128)S(1)} %get-tuple-element.144), channel_id=1, source_target_pairs={{4,0},{8,4},{12,8},{16,12},{20,16},{24,20},{28,24},{32,28},{36,32}... | collective-permute-start | bytes 584 | tf_op jit(solution)/shard_map/ppermute | solution.py:23
  86.8 1.3 collective-permute-start.10
  88.1 4.0 %collective-permute-start.9 = (f32[3,1,2048]{2,1,0:T(1,128)S(1)}, f32[3,1,2048]{2,1,0:T(1,128)S(1)}, u32[]{:S(2)}, u32[]{:S(2)}) collective-permute-start(f32[3,1,2048]{2,1,0:T(1,128)S(1)} %get-tuple-element.146), channel_id=1, source_target_pairs={{0,1},{1,2},{2,3},{4,5},{5,6},{6,7},{8,9},{9,10},{10,11},{12,13},{... | collective-permute-start | bytes 73736 | tf_op jit(solution)/shard_map/ppermute | solution.py:22
  92.1 3.5 %collective-permute-start.7 = (f32[3,8,2]{2,1,0:T(8,128)S(1)}, f32[3,8,2]{2,1,0:T(8,128)S(1)}, u32[]{:S(2)}, u32[]{:S(2)}) collective-permute-start(f32[3,8,2]{2,1,0:T(8,128)S(1)} %get-tuple-element.145), channel_id=1, source_target_pairs={{0,4},{4,8},{8,12},{12,16},{16,20},{20,24},{24,28},{28,32},{32,36}... | collective-permute-start | bytes 584 | tf_op jit(solution)/shard_map/ppermute | solution.py:22
  95.8 0.7 collective-permute-done.7
  97.0 7.1 %collective-permute-start.11 = (f32[29,2]{1,0:T(8,128)S(1)}, f32[29,2]{1,0:T(8,128)S(1)}, u32[]{:S(2)}, u32[]{:S(2)}) collective-permute-start(f32[29,2]{1,0:T(8,128)S(1)} %get-tuple-element.132), channel_id=1, source_target_pairs={{4,0},{8,4},{12,8},{16,12},{20,16},{24,20},{28,24},{32,28},{36,32}... | collective-permute-start | bytes 704 | tf_op jit(solution)/shard_map/ppermute | solution.py:23
  104.2 1.9 %collective-permute-start.12 = (f32[29,2]{1,0:T(8,128)S(1)}, f32[29,2]{1,0:T(8,128)S(1)}, u32[]{:S(2)}, u32[]{:S(2)}) collective-permute-start(f32[29,2]{1,0:T(8,128)S(1)} %get-tuple-element.133), channel_id=1, source_target_pairs={{0,4},{4,8},{8,12},{12,16},{16,20},{20,24},{24,28},{28,32},{32,36}... | collective-permute-start | bytes 704 | tf_op jit(solution)/shard_map/ppermute | solution.py:22
  106.1 1.3 collective-permute-start.13
  107.4 4.0 %collective-permute-start.14 = (f32[3,1,2048]{2,1,0:T(1,128)S(1)}, f32[3,1,2048]{2,1,0:T(1,128)S(1)}, u32[]{:S(2)}, u32[]{:S(2)}) collective-permute-start(f32[3,1,2048]{2,1,0:T(1,128)S(1)} %get-tuple-element.143), channel_id=1, source_target_pairs={{0,1},{1,2},{2,3},{4,5},{5,6},{6,7},{8,9},{9,10},{10,11},{12,13},{... | collective-permute-start | bytes 73736 | tf_op jit(solution)/shard_map/ppermute | solution.py:22
  111.6 0.8 collective-permute-done.14
  112.8 1.9 %collective-permute-start.15 = (bf16[24,512]{1,0:T(8,128)(2,1)S(1)}, bf16[24,512]{1,0:T(8,128)(2,1)S(1)}, u32[]{:S(2)}, u32[]{:S(2)}) collective-permute-start(bf16[24,512]{1,0:T(8,128)(2,1)S(1)} %get-tuple-element.141), channel_id=1, source_target_pairs={{496,0},{500,4},{504,8},{508,12},{0,16},{4,20},{8,24},{12,28},{16,... | collective-permute-start | bytes 73736 | tf_op jit(solution)/shard_map/ppermute | solution.py:12
  114.7 4.9 %compare_and_fusion = (pred[2048]{0:T(1024)(128)(4,1)S(1)}, s32[2048]{0:T(1024)S(1)}) fusion(s32[]{:T(128)} %bitcast.30, s32[]{:T(128)} %bitcast.29, s32[]{:T(128)} %bitcast.28, s32[]{:T(128)} %bitcast.27, s32[]{:T(128)} %bitcast.26, s32[]{:T(128)} %bitcast.25, s32[]{:T(128)} %bitcast.24, s32[]{:T(128)} %bitcast.23, u32[2048]{0:T(1024)S(1)} %get-tuple-element.67), kind=kLoop, calls=%fused_computation.138 | loop fusion | flops 63488 | bytes 18464 | tf_op jit(solution)/shard_map/jit(_take)/and | solution.py:126
  119.6 1.9 %collective-permute-start.16 = (bf16[24,512]{1,0:T(8,128)(2,1)S(1)}, bf16[24,512]{1,0:T(8,128)(2,1)S(1)}, u32[]{:S(2)}, u32[]{:S(2)}) collective-permute-start(bf16[24,512]{1,0:T(8,128)(2,1)S(1)} %get-tuple-element.140), channel_id=1, source_target_pairs={{500,0},{504,4},{508,8},{0,12},{4,16},{8,20},{12,24},{16,28},{20,3... | collective-permute-start | bytes 73736 | tf_op jit(solution)/shard_map/ppermute | solution.py:12
  121.5 1.9 %collective-permute-start.17 = (bf16[24,512]{1,0:T(8,128)(2,1)S(1)}, bf16[24,512]{1,0:T(8,128)(2,1)S(1)}, u32[]{:S(2)}, u32[]{:S(2)}) collective-permute-start(bf16[24,512]{1,0:T(8,128)(2,1)S(1)} %get-tuple-element.139), channel_id=1, source_target_pairs={{504,0},{508,4},{0,8},{4,12},{8,16},{12,20},{16,24},{20,28},{24,32... | collective-permute-start | bytes 73736 | tf_op jit(solution)/shard_map/ppermute | solution.py:12
  123.5 2.4 %collective-permute-start.18 = (bf16[24,512]{1,0:T(8,128)(2,1)S(1)}, bf16[24,512]{1,0:T(8,128)(2,1)S(1)}, u32[]{:S(2)}, u32[]{:S(2)}) collective-permute-start(bf16[24,512]{1,0:T(8,128)(2,1)S(1)} %get-tuple-element.138), channel_id=1, source_target_pairs={{508,0},{0,4},{4,8},{8,12},{12,16},{16,20},{20,24},{24,28},{28,32}... | collective-permute-start | bytes 73736 | tf_op jit(solution)/shard_map/ppermute | solution.py:12
  125.9 2.2 %collective-permute-done.16 = bf16[24,512]{1,0:T(8,128)(2,1)S(1)} collective-permute-done((bf16[24,512]{1,0:T(8,128)(2,1)S(1)}, bf16[24,512]{1,0:T(8,128)(2,1)S(1)}, u32[]{:S(2)}, u32[]{:S(2)}) %collective-permute-start.16) | collective-permute-done | bytes 24608 | tf_op jit(solution)/shard_map/ppermute | solution.py:12
  128.1 1.4 collective-permute-done.17
  129.5 6.0 %collective-permute-start.19 = (bf16[24,512]{1,0:T(8,128)(2,1)S(1)}, bf16[24,512]{1,0:T(8,128)(2,1)S(1)}, u32[]{:S(2)}, u32[]{:S(2)}) collective-permute-start(bf16[24,512]{1,0:T(8,128)(2,1)S(1)} %get-tuple-element.136), channel_id=1, source_target_pairs={{4,0},{8,4},{12,8},{16,12},{20,16},{24,20},{28,24},{32,28},{36,32}... | collective-permute-start | bytes 73736 | tf_op jit(solution)/shard_map/ppermute | solution.py:12
  135.5 3.6 %collective-permute-start.20 = (bf16[24,512]{1,0:T(8,128)(2,1)S(1)}, bf16[24,512]{1,0:T(8,128)(2,1)S(1)}, u32[]{:S(2)}, u32[]{:S(2)}) collective-permute-start(bf16[24,512]{1,0:T(8,128)(2,1)S(1)} %get-tuple-element.135), channel_id=1, source_target_pairs={{8,0},{12,4},{16,8},{20,12},{24,16},{28,20},{32,24},{36,28},{40,32... | collective-permute-start | bytes 73736 | tf_op jit(solution)/shard_map/ppermute | solution.py:12
  139.2 3.3 %collective-permute-start.21 = (bf16[24,512]{1,0:T(8,128)(2,1)S(1)}, bf16[24,512]{1,0:T(8,128)(2,1)S(1)}, u32[]{:S(2)}, u32[]{:S(2)}) collective-permute-start(bf16[24,512]{1,0:T(8,128)(2,1)S(1)} %get-tuple-element.134), channel_id=1, source_target_pairs={{12,0},{16,4},{20,8},{24,12},{28,16},{32,20},{36,24},{40,28},{44,3... | collective-permute-start | bytes 73736 | tf_op jit(solution)/shard_map/ppermute | solution.py:12
  142.5 2.8 %collective-permute-done.21 = bf16[24,512]{1,0:T(8,128)(2,1)S(1)} collective-permute-done((bf16[24,512]{1,0:T(8,128)(2,1)S(1)}, bf16[24,512]{1,0:T(8,128)(2,1)S(1)}, u32[]{:S(2)}, u32[]{:S(2)}) %collective-permute-start.21) | collective-permute-done | bytes 24608 | tf_op jit(solution)/shard_map/ppermute | solution.py:12
  145.2 2.8 %fusion.8 = f32[24,8,512]{2,0,1:T(8,128)S(1)} fusion(bf16[8,24,512]{2,1,0:T(8,128)(2,1)S(1)} %constant_dynamic-update-slice_fusion.3, bf16[1,8,512,512]{3,2,1,0:T(8,128)(2,1)} %param.13), kind=kOutput, calls=%fused_computation.11 | convolution fusion | flops 100663296 | bytes 4784128 | tf_op jit(solution)/shard_map/dfw,dwc->fdc/dot_general | solution.py:125
  148.7 5.5 %gather_fusion.1 = f32[2048,24]{1,0:T(8,128)S(1)} fusion(f32[24,4096]{0,1:T(8,128)S(1)} %bitcast.153, s32[2048]{0:T(1024)S(1)} %broadcast_clamp_fusion.1), kind=kCustom, calls=%fused_computation.1 | custom fusion | bytes 401408 | tf_op jit(solution)/shard_map/jit(_take)/gather | solution.py:126
  154.5 0.7 bitcast_select_fusion
  (80 shorter events, 4.1 us)
Async XLA Ops:
  16.4 50.7 %copy-start.1 = (f32[2048]{0:T(1024)S(1)}, f32[2048]{0:T(1024)}, u32[]{:S(2)}) copy-start(f32[2048]{0:T(1024)} %param.15) | copy-start | bytes 24580
  16.4 50.7 %copy-start.2 = (f32[2048]{0:T(1024)S(1)}, f32[2048]{0:T(1024)}, u32[]{:S(2)}) copy-start(f32[2048]{0:T(1024)} %param.16) | copy-start | bytes 24580
  16.4 50.7 %copy-start.3 = (s32[2048]{0:T(1024)S(1)}, s32[2048]{0:T(1024)}, u32[]{:S(2)}) copy-start(s32[2048]{0:T(1024)} %param.17) | copy-start | bytes 24580
  16.4 50.7 %copy-start.4 = (f32[3]{0:T(128)S(1)}, f32[3]{0:T(128)}, u32[]{:S(2)}) copy-start(f32[3]{0:T(128)} %param.14) | copy-start | bytes 40
  20.3 46.8 %collective-permute-start = (f32[48,512]{1,0:T(8,128)S(1)}, f32[48,512]{1,0:T(8,128)S(1)}, u32[]{:S(2)}, u32[]{:S(2)}) collective-permute-start(f32[48,512]{1,0:T(8,128)S(1)} %get-tuple-element.123), channel_id=1, source_target_pairs={{16,0},{20,4},{24,8},{28,12},{32,16},{36,20},{40,24},{44,28},{48,3... | collective-permute-start | bytes 294920 | tf_op jit(solution)/shard_map/ppermute | solution.py:12
  35.2 32.0 %collective-permute-start.1 = (f32[48,512]{1,0:T(8,128)S(1)}, f32[48,512]{1,0:T(8,128)S(1)}, u32[]{:S(2)}, u32[]{:S(2)}) collective-permute-start(f32[48,512]{1,0:T(8,128)S(1)} %get-tuple-element.122), channel_id=1, source_target_pairs={{12,0},{16,4},{20,8},{24,12},{28,16},{32,20},{36,24},{40,28},{44,3... | collective-permute-start | bytes 294920 | tf_op jit(solution)/shard_map/ppermute | solution.py:12
  38.7 28.6 %collective-permute-start.2 = (f32[48,512]{1,0:T(8,128)S(1)}, f32[48,512]{1,0:T(8,128)S(1)}, u32[]{:S(2)}, u32[]{:S(2)}) collective-permute-start(f32[48,512]{1,0:T(8,128)S(1)} %get-tuple-element.121), channel_id=1, source_target_pairs={{8,0},{12,4},{16,8},{20,12},{24,16},{28,20},{32,24},{36,28},{40,32... | collective-permute-start | bytes 294920 | tf_op jit(solution)/shard_map/ppermute | solution.py:12
  41.3 26.0 %collective-permute-start.3 = (f32[48,512]{1,0:T(8,128)S(1)}, f32[48,512]{1,0:T(8,128)S(1)}, u32[]{:S(2)}, u32[]{:S(2)}) collective-permute-start(f32[48,512]{1,0:T(8,128)S(1)} %get-tuple-element.120), channel_id=1, source_target_pairs={{4,0},{8,4},{12,8},{16,12},{20,16},{24,20},{28,24},{32,28},{36,32}... | collective-permute-start | bytes 294920 | tf_op jit(solution)/shard_map/ppermute | solution.py:12
  67.3 8.2 %collective-permute-start.4 = (f32[48,512]{1,0:T(8,128)S(1)}, f32[48,512]{1,0:T(8,128)S(1)}, u32[]{:S(2)}, u32[]{:S(2)}) collective-permute-start(f32[48,512]{1,0:T(8,128)S(1)} %get-tuple-element.118), channel_id=1, source_target_pairs={{508,0},{0,4},{4,8},{8,12},{12,16},{16,20},{20,24},{24,28},{28,32}... | collective-permute-start | bytes 294920 | tf_op jit(solution)/shard_map/ppermute | solution.py:12
  70.2 9.9 %collective-permute-start.5 = (f32[48,512]{1,0:T(8,128)S(1)}, f32[48,512]{1,0:T(8,128)S(1)}, u32[]{:S(2)}, u32[]{:S(2)}) collective-permute-start(f32[48,512]{1,0:T(8,128)S(1)} %get-tuple-element.117), channel_id=1, source_target_pairs={{504,0},{508,4},{0,8},{4,12},{8,16},{12,20},{16,24},{20,28},{24,32... | collective-permute-start | bytes 294920 | tf_op jit(solution)/shard_map/ppermute | solution.py:12
  72.8 11.0 %collective-permute-start.6 = (f32[48,512]{1,0:T(8,128)S(1)}, f32[48,512]{1,0:T(8,128)S(1)}, u32[]{:S(2)}, u32[]{:S(2)}) collective-permute-start(f32[48,512]{1,0:T(8,128)S(1)} %get-tuple-element.116), channel_id=1, source_target_pairs={{500,0},{504,4},{508,8},{0,12},{4,16},{8,20},{12,24},{16,28},{20,3... | collective-permute-start | bytes 294920 | tf_op jit(solution)/shard_map/ppermute | solution.py:12
  84.2 11.6 %collective-permute-start.8 = (f32[3,8,2]{2,1,0:T(8,128)S(1)}, f32[3,8,2]{2,1,0:T(8,128)S(1)}, u32[]{:S(2)}, u32[]{:S(2)}) collective-permute-start(f32[3,8,2]{2,1,0:T(8,128)S(1)} %get-tuple-element.144), channel_id=1, source_target_pairs={{4,0},{8,4},{12,8},{16,12},{20,16},{24,20},{28,24},{32,28},{36,32}... | collective-permute-start | bytes 584 | tf_op jit(solution)/shard_map/ppermute | solution.py:23
  86.8 9.6 %collective-permute-start.10 = (f32[3,1,2048]{2,1,0:T(1,128)S(1)}, f32[3,1,2048]{2,1,0:T(1,128)S(1)}, u32[]{:S(2)}, u32[]{:S(2)}) collective-permute-start(f32[3,1,2048]{2,1,0:T(1,128)S(1)} %get-tuple-element.147), channel_id=1, source_target_pairs={{1,0},{2,1},{3,2},{5,4},{6,5},{7,6},{9,8},{10,9},{11,10},{13,12},{... | collective-permute-start | bytes 73736 | tf_op jit(solution)/shard_map/ppermute | solution.py:23
  88.1 8.4 %collective-permute-start.9 = (f32[3,1,2048]{2,1,0:T(1,128)S(1)}, f32[3,1,2048]{2,1,0:T(1,128)S(1)}, u32[]{:S(2)}, u32[]{:S(2)}) collective-permute-start(f32[3,1,2048]{2,1,0:T(1,128)S(1)} %get-tuple-element.146), channel_id=1, source_target_pairs={{0,1},{1,2},{2,3},{4,5},{5,6},{6,7},{8,9},{9,10},{10,11},{12,13},{... | collective-permute-start | bytes 73736 | tf_op jit(solution)/shard_map/ppermute | solution.py:22
  92.1 4.3 %collective-permute-start.7 = (f32[3,8,2]{2,1,0:T(8,128)S(1)}, f32[3,8,2]{2,1,0:T(8,128)S(1)}, u32[]{:S(2)}, u32[]{:S(2)}) collective-permute-start(f32[3,8,2]{2,1,0:T(8,128)S(1)} %get-tuple-element.145), channel_id=1, source_target_pairs={{0,4},{4,8},{8,12},{12,16},{16,20},{20,24},{24,28},{28,32},{32,36}... | collective-permute-start | bytes 584 | tf_op jit(solution)/shard_map/ppermute | solution.py:22
  96.8 51.3 %copy-start = (f32[3,8,2048]{2,1,0:T(8,128)}, f32[3,8,2048]{2,1,0:T(8,128)S(1)}, u32[]{:S(2)}) copy-start(f32[3,8,2048]{2,1,0:T(8,128)S(1)} %fusion.27) | copy-start | bytes 589828
  97.0 14.4 %collective-permute-start.11 = (f32[29,2]{1,0:T(8,128)S(1)}, f32[29,2]{1,0:T(8,128)S(1)}, u32[]{:S(2)}, u32[]{:S(2)}) collective-permute-start(f32[29,2]{1,0:T(8,128)S(1)} %get-tuple-element.132), channel_id=1, source_target_pairs={{4,0},{8,4},{12,8},{16,12},{20,16},{24,20},{28,24},{32,28},{36,32}... | collective-permute-start | bytes 704 | tf_op jit(solution)/shard_map/ppermute | solution.py:23
  104.2 7.2 %collective-permute-start.12 = (f32[29,2]{1,0:T(8,128)S(1)}, f32[29,2]{1,0:T(8,128)S(1)}, u32[]{:S(2)}, u32[]{:S(2)}) collective-permute-start(f32[29,2]{1,0:T(8,128)S(1)} %get-tuple-element.133), channel_id=1, source_target_pairs={{0,4},{4,8},{8,12},{12,16},{16,20},{20,24},{24,28},{28,32},{32,36}... | collective-permute-start | bytes 704 | tf_op jit(solution)/shard_map/ppermute | solution.py:22
  106.1 5.5 %collective-permute-start.13 = (f32[3,1,2048]{2,1,0:T(1,128)S(1)}, f32[3,1,2048]{2,1,0:T(1,128)S(1)}, u32[]{:S(2)}, u32[]{:S(2)}) collective-permute-start(f32[3,1,2048]{2,1,0:T(1,128)S(1)} %get-tuple-element.142), channel_id=1, source_target_pairs={{1,0},{2,1},{3,2},{5,4},{6,5},{7,6},{9,8},{10,9},{11,10},{13,12},{... | collective-permute-start | bytes 73736 | tf_op jit(solution)/shard_map/ppermute | solution.py:23
  107.4 4.9 %collective-permute-start.14 = (f32[3,1,2048]{2,1,0:T(1,128)S(1)}, f32[3,1,2048]{2,1,0:T(1,128)S(1)}, u32[]{:S(2)}, u32[]{:S(2)}) collective-permute-start(f32[3,1,2048]{2,1,0:T(1,128)S(1)} %get-tuple-element.143), channel_id=1, source_target_pairs={{0,1},{1,2},{2,3},{4,5},{5,6},{6,7},{8,9},{9,10},{10,11},{12,13},{... | collective-permute-start | bytes 73736 | tf_op jit(solution)/shard_map/ppermute | solution.py:22
  112.8 13.1 %collective-permute-start.15 = (bf16[24,512]{1,0:T(8,128)(2,1)S(1)}, bf16[24,512]{1,0:T(8,128)(2,1)S(1)}, u32[]{:S(2)}, u32[]{:S(2)}) collective-permute-start(bf16[24,512]{1,0:T(8,128)(2,1)S(1)} %get-tuple-element.141), channel_id=1, source_target_pairs={{496,0},{500,4},{504,8},{508,12},{0,16},{4,20},{8,24},{12,28},{16,... | collective-permute-start | bytes 73736 | tf_op jit(solution)/shard_map/ppermute | solution.py:12
  119.6 8.5 %collective-permute-start.16 = (bf16[24,512]{1,0:T(8,128)(2,1)S(1)}, bf16[24,512]{1,0:T(8,128)(2,1)S(1)}, u32[]{:S(2)}, u32[]{:S(2)}) collective-permute-start(bf16[24,512]{1,0:T(8,128)(2,1)S(1)} %get-tuple-element.140), channel_id=1, source_target_pairs={{500,0},{504,4},{508,8},{0,12},{4,16},{8,20},{12,24},{16,28},{20,3... | collective-permute-start | bytes 73736 | tf_op jit(solution)/shard_map/ppermute | solution.py:12
  121.5 7.9 %collective-permute-start.17 = (bf16[24,512]{1,0:T(8,128)(2,1)S(1)}, bf16[24,512]{1,0:T(8,128)(2,1)S(1)}, u32[]{:S(2)}, u32[]{:S(2)}) collective-permute-start(bf16[24,512]{1,0:T(8,128)(2,1)S(1)} %get-tuple-element.139), channel_id=1, source_target_pairs={{504,0},{508,4},{0,8},{4,12},{8,16},{12,20},{16,24},{20,28},{24,32... | collective-permute-start | bytes 73736 | tf_op jit(solution)/shard_map/ppermute | solution.py:12
  123.5 6.0 %collective-permute-start.18 = (bf16[24,512]{1,0:T(8,128)(2,1)S(1)}, bf16[24,512]{1,0:T(8,128)(2,1)S(1)}, u32[]{:S(2)}, u32[]{:S(2)}) collective-permute-start(bf16[24,512]{1,0:T(8,128)(2,1)S(1)} %get-tuple-element.138), channel_id=1, source_target_pairs={{508,0},{0,4},{4,8},{8,12},{12,16},{16,20},{20,24},{24,28},{28,32}... | collective-permute-start | bytes 73736 | tf_op jit(solution)/shard_map/ppermute | solution.py:12
  129.5 13.0 %collective-permute-start.19 = (bf16[24,512]{1,0:T(8,128)(2,1)S(1)}, bf16[24,512]{1,0:T(8,128)(2,1)S(1)}, u32[]{:S(2)}, u32[]{:S(2)}) collective-permute-start(bf16[24,512]{1,0:T(8,128)(2,1)S(1)} %get-tuple-element.136), channel_id=1, source_target_pairs={{4,0},{8,4},{12,8},{16,12},{20,16},{24,20},{28,24},{32,28},{36,32}... | collective-permute-start | bytes 73736 | tf_op jit(solution)/shard_map/ppermute | solution.py:12
  135.5 7.0 %collective-permute-start.20 = (bf16[24,512]{1,0:T(8,128)(2,1)S(1)}, bf16[24,512]{1,0:T(8,128)(2,1)S(1)}, u32[]{:S(2)}, u32[]{:S(2)}) collective-permute-start(bf16[24,512]{1,0:T(8,128)(2,1)S(1)} %get-tuple-element.135), channel_id=1, source_target_pairs={{8,0},{12,4},{16,8},{20,12},{24,16},{28,20},{32,24},{36,28},{40,32... | collective-permute-start | bytes 73736 | tf_op jit(solution)/shard_map/ppermute | solution.py:12
  139.2 6.1 %collective-permute-start.21 = (bf16[24,512]{1,0:T(8,128)(2,1)S(1)}, bf16[24,512]{1,0:T(8,128)(2,1)S(1)}, u32[]{:S(2)}, u32[]{:S(2)}) collective-permute-start(bf16[24,512]{1,0:T(8,128)(2,1)S(1)} %get-tuple-element.134), channel_id=1, source_target_pairs={{12,0},{16,4},{20,8},{24,12},{28,16},{32,20},{36,24},{40,28},{44,3... | collective-permute-start | bytes 73736 | tf_op jit(solution)/shard_map/ppermute | solution.py:12
where the time goes:
time: 157 us; the launch traced here: 155 us
  starting transfers between devices  78.6 us (50%)
  other arithmetic  29.4 us (19%)
  local copies, waits for them, and re-layouts  23.4 us (15%)
  waiting for transfers between devices  16 us (10%)
  matrix products  6.36 us (4%)
    ppermute x14, starting transfers between devices, from_behind(): return lax.ppermute(block, axis, route)  52.9 us
    select_n x4, other arithmetic, column_slots(): owner = jnp.searchsorted(group_end, columns, side='right')  19.6 us
    ppermute x14, waiting for transfers between devices, from_behind(): return lax.ppermute(block, axis, route)  14.6 us
    ppermute x4, starting transfers between devices, padded(): before = lax.ppermute(last, axis, up)  13.4 us
    gather x2, local copies, waits for them, and re-layouts, shards(): jnp.take(fields, slot_index.reshape(-1), axis=1)  12.5 us
    ppermute x4, starting transfers between devices, padded(): after = lax.ppermute(leading, axis, down)  12.3 us
    gather x2, local copies, waits for them, and re-layouts, shards(): grad_outer = jnp.take(slot_grad.reshape(field_rows, -1), back_index, axis=1)  5.77 us
    and x1, other arithmetic, shards(): grad_outer = jnp.take(slot_grad.reshape(field_rows, -1), back_index, axis=1)  4.91 us
  transfers between devices with their start and end apart: 22, of which 7 were waited for; matrix products, arithmetic and copies ran while one was open for 18% of the time, Pallas kernels for 0%

commit v1 on v0

v1 whole, which is shorter than its diff:
```python
import functools

import jax
import jax.numpy as jnp
from jax import lax
from jax.experimental import pallas as pl
from jax.experimental.pallas import tpu as pltpu
from jax.sharding import PartitionSpec as P

MESH = pl.DeviceIdType.MESH
LANES = 128
HALO = 2
SEND_ORDER = (0, 7, 1, 6, 2, 5, 3, 4)


def kernel(
    n_tile,
    n_lev,
    traj_ref,
    inc_ref,
    counts_ref,
    kappa_ref,
    courant_ref,
    vertical_ref,
    offset_ref,
    weight_hbm,
    tangent_out,
    grad_out,
    weight,
    shifted,
    fields,
    outgoing,
    recv,
    coef,
    delta,
    loss,
    tang,
    up_out,
    down_out,
    below_in,
    above_in,
    adj,
    back,
    placed,
    weight_sem,
    fwd_send,
    fwd_recv,
    coef_send,
    coef_recv,
    col_send,
    col_recv,
    lev_send,
    lev_recv,
    ret_send,
    ret_recv,
):
    tracers, levels, cols = traj_ref.shape
    rows = tracers * levels
    reach = weight_hbm.shape[1]
    win, cap = weight_hbm.shape[2], weight_hbm.shape[3]
    centre = reach // 2
    span = cols // reach
    tiles = cols // LANES
    sub = span // LANES
    me = lax.axis_index("tile")
    lev = lax.axis_index("lev")

    def tile_at(distance):
        return (lax.rem(me + (n_tile + distance), n_tile), lev)

    weight_copies = [
        pltpu.make_async_copy(weight_hbm.at[0, d], weight.at[d], weight_sem.at[d]) for d in range(reach)
    ]
    for d in SEND_ORDER:
        weight_copies[d].start()

    barrier = pltpu.get_barrier_semaphore()
    for distance in range(-centre, centre + 1):
        if distance != 0:
            pl.semaphore_signal(barrier, inc=1, device_id=tile_at(distance), device_id_type=MESH)

    @pl.when(lev > 0)
    def _():
        pl.semaphore_signal(barrier, inc=1, device_id=(me, lev - 1), device_id_type=MESH)

    @pl.when(lev < n_lev - 1)
    def _():
        pl.semaphore_signal(barrier, inc=1, device_id=(me, lev + 1), device_id_type=MESH)

    stacked = jnp.concatenate(
        [ref[m].astype(jnp.float32) for ref in (traj_ref, inc_ref) for m in range(tracers)], axis=0
    ).astype(jnp.bfloat16)
    for t in range(tiles):
        fields[t] = stacked[:, t * LANES : (t + 1) * LANES]
    for t in range(tiles, fields.shape[0]):
        fields[t] = jnp.zeros((2 * rows, LANES), jnp.bfloat16)
    vertical = vertical_ref[...]
    coef[pl.ds(0, 1), pl.ds(LANES, cols)] = courant_ref[...]
    coef[pl.ds(1, 1), pl.ds(LANES, cols)] = offset_ref[...].astype(jnp.float32)
    coef[pl.ds(2, 1), pl.ds(LANES, cols)] = jnp.maximum(vertical, 0.0)
    coef[pl.ds(3, 1), pl.ds(LANES, cols)] = jnp.maximum(-vertical, 0.0)
    coef[pl.ds(4, 4), pl.ds(LANES, cols)] = jnp.zeros((4, cols), jnp.float32)
    up_out[pl.ds(6, 2), :] = jnp.zeros((2, cols), jnp.float32)
    down_out[pl.ds(6, 2), :] = jnp.zeros((2, cols), jnp.float32)

    @pl.when(lev == 0)
    def _():
        below_in[...] = jnp.zeros_like(below_in)

    @pl.when(lev == n_lev - 1)
    def _():
        above_in[...] = jnp.zeros_like(above_in)

    placed[:, pl.ds(0, 1)] = jnp.zeros((reach, 1, rows, LANES), jnp.float32)
    placed[:, pl.ds(placed.shape[1] - 1, 1)] = jnp.zeros((reach, 1, rows, LANES), jnp.float32)

    starts = []
    total = jnp.int32(0)
    for d in range(reach):
        starts.append(total)
        total = total + counts_ref[0, d]

    firsts = [lax.shift_right_logical(start, 7) for start in starts]
    shifts = [lax.bitwise_and(start, LANES - 1) for start in starts]
    parts = cap // LANES
    lane = lax.broadcasted_iota(jnp.int32, (2 * rows, LANES), 1)
    skew = lax.broadcasted_iota(jnp.int32, (2 * LANES, LANES), 0) - lax.broadcasted_iota(
        jnp.int32, (2 * LANES, LANES), 1
    )

    def selection(amount):
        return jnp.where(skew == amount, 1.0, 0.0).astype(jnp.bfloat16)

    def slots_of(d):
        loaded = [fields[firsts[d] + t] for t in range(parts + 1)]
        pairs = [jnp.concatenate([loaded[t], loaded[t + 1]], axis=1) for t in range(parts)]
        moved = jnp.dot(
            jnp.concatenate(pairs, axis=0), selection(shifts[d]), preferred_element_type=jnp.float32
        )
        pieces = []
        for t in range(parts):
            value = moved[t * 2 * rows : (t + 1) * 2 * rows]
            pieces.append(jnp.where(lane + t * LANES < counts_ref[0, d], value, 0.0).astype(jnp.bfloat16))
        return jnp.concatenate(pieces, axis=1)

    tall = lax.broadcasted_iota(jnp.int32, (win, LANES), 1)

    def place_weight(d):
        chosen = selection(LANES - shifts[d])
        nothing = jnp.zeros((win, LANES), jnp.bfloat16)
        live = []
        for t in range(parts):
            piece = weight[d, :, pl.ds(t * LANES, LANES)]
            live.append(jnp.where(tall + t * LANES < counts_ref[0, d], piece, nothing))
        live = [nothing, *live, nothing]
        for t in range(parts + 1):
            moved = jnp.dot(
                jnp.concatenate([live[t], live[t + 1]], axis=1), chosen, preferred_element_type=jnp.float32
            )
            shifted[d, :, pl.ds(t * LANES, LANES)] = moved.astype(jnp.bfloat16)

    forward = {
        d: pltpu.make_async_remote_copy(
            src_ref=outgoing.at[d],
            dst_ref=recv.at[d],
            send_sem=fwd_send.at[d],
            recv_sem=fwd_recv.at[d],
            device_id=tile_at(d - centre),
            device_id_type=MESH,
        )
        for d in range(reach)
        if d != centre
    }
    giving = {
        d: pltpu.make_async_remote_copy(
            src_ref=adj.at[:, pl.ds(d * span, win)],
            dst_ref=back.at[d],
            send_sem=ret_send.at[d],
            recv_sem=ret_recv.at[d],
            device_id=tile_at(centre - d),
            device_id_type=MESH,
        )
        for d in range(reach)
        if d != centre
    }

    def edges(ref, send_sem, recv_sem, base):
        left = pltpu.make_async_remote_copy(
            src_ref=ref.at[:, pl.ds(LANES, LANES)],
            dst_ref=ref.at[:, pl.ds(LANES + cols, LANES)],
            send_sem=send_sem.at[base],
            recv_sem=recv_sem.at[base],
            device_id=tile_at(-1),
            device_id_type=MESH,
        )
        right = pltpu.make_async_remote_copy(
            src_ref=ref.at[:, pl.ds(cols, LANES)],
            dst_ref=ref.at[:, pl.ds(0, LANES)],
            send_sem=send_sem.at[base + 1],
            recv_sem=recv_sem.at[base + 1],
            device_id=tile_at(1),
            device_id_type=MESH,
        )
        return left, right

    coef_edges = edges(coef, coef_send, coef_recv, 0)
    delta_edges = edges(delta, col_send, col_recv, 0)
    tang_edges = edges(tang, col_send, col_recv, 2)

    stage_ranges = (
        ((0, 1), (tiles - 1, tiles)),
        ((1, 5), (11, tiles - 1)),
        ((5, 11),),
    )
    level_up, level_down = {}, {}
    index = 0
    for ranges in stage_ranges:
        for lo, hi in ranges:
            part = pl.ds(lo * LANES, (hi - lo) * LANES)
            level_up[lo, hi] = pltpu.make_async_remote_copy(
                src_ref=up_out.at[:, part],
                dst_ref=below_in.at[:, part],
                send_sem=lev_send.at[index],
                recv_sem=lev_recv.at[index],
                device_id=(me, lax.rem(lev + 1, n_lev)),
                device_id_type=MESH,
            )
            level_down[lo, hi] = pltpu.make_async_remote_copy(
                src_ref=down_out.at[:, part],
                dst_ref=above_in.at[:, part],
                send_sem=lev_send.at[index + 1],
                recv_sem=lev_recv.at[index + 1],
                device_id=(me, lax.rem(lev + n_lev - 1, n_lev)),
                device_id_type=MESH,
            )
            index += 2

    def level_start(stage):
        @pl.when(lev < n_lev - 1)
        def _():
            for key in stage_ranges[stage]:
                level_up[key].start()

        @pl.when(lev > 0)
        def _():
            for key in stage_ranges[stage]:
                level_down[key].start()

    def level_wait(stage):
        @pl.when(lev > 0)
        def _():
            for key in stage_ranges[stage]:
                level_up[key].wait_recv()

        @pl.when(lev < n_lev - 1)
        def _():
            for key in stage_ranges[stage]:
                level_down[key].wait_recv()

    for position, d in enumerate(SEND_ORDER):
        slotted = slots_of(d)
        weight_copies[d].wait()
        window = lax.dot_general(
            slotted, weight[d], (((1,), (1,)), ((), ())), preferred_element_type=jnp.float32
        )
        if d == centre:
            recv[d] = window
        else:
            outgoing[d] = window
            if position == 0:
                pl.semaphore_wait(
                    barrier,
                    2 * centre + (lev > 0).astype(jnp.int32) + (lev < n_lev - 1).astype(jnp.int32),
                )
            forward[d].start()
            if position == 0:
                for copy in coef_edges:
                    copy.start()

    def finish_block(b):
        value = recv[b, :, pl.ds(0, span)] + recv[(b - 1) % reach, :, pl.ds(span, span)]
        for m in range(tracers):
            part = pl.ds(m * levels, levels)
            loss[part, pl.ds(b * span, span)] = 2.0 * kappa_ref[m] * value[m * levels : (m + 1) * levels]
        delta[:, pl.ds(LANES + b * span, span)] = value[rows:]

    def level_rows(width):
        return lax.broadcasted_iota(jnp.int32, (levels, width), 0)

    def tangent_partial(lo, hi):
        width = (hi - lo) * LANES
        own = pl.ds(LANES + lo * LANES, width)
        courant, offset = coef[pl.ds(0, 1), own], coef[pl.ds(1, 1), own]
        rising, sinking = coef[pl.ds(2, 1), own], coef[pl.ds(3, 1), own]
        level = level_rows(width)
        for m in range(tracers):
            part = pl.ds(m * levels, levels)
            wide = delta[part, pl.ds(lo * LANES, width + 2 * LANES)]
            here = wide[:, LANES : LANES + width]
            departed = jnp.zeros_like(here)
            for shift in range(-HALO, HALO + 1):
                moved = here
                if shift != 0:
                    moved = pltpu.roll(wide, (-shift) % (width + 2 * LANES), 1)[:, LANES : LANES + width]
                departed = jnp.where(offset == float(shift), moved, departed)
            below = jnp.where(level == 0, 0.0, pltpu.roll(here, 1, 0))
            above = jnp.where(level == levels - 1, 0.0, pltpu.roll(here, levels - 1, 0))
            value = (
                here
                + courant * (departed - here)
                + rising * (below - here)
                + sinking * (above - here)
                - loss[part, pl.ds(lo * LANES, width)] * here
            )
            tang[part, own] = value
            out = pl.ds(lo * LANES, width)
            up_out[pl.ds(m, 1), out] = value[levels - 1 : levels]
            up_out[pl.ds(tracers + m, 1), out] = here[levels - 1 : levels]
            down_out[pl.ds(m, 1), out] = value[0:1]
            down_out[pl.ds(tracers + m, 1), out] = here[0:1]

    def tangent_finish(lo, hi):
        width = (hi - lo) * LANES
        own = pl.ds(LANES + lo * LANES, width)
        out = pl.ds(lo * LANES, width)
        rising, sinking = coef[pl.ds(2, 1), own], coef[pl.ds(3, 1), own]
        level = level_rows(width)
        for m in range(tracers):
            part = pl.ds(m * levels, levels)
            value = tang[part, own]
            value = value + jnp.where(level == 0, rising * below_in[pl.ds(tracers + m, 1), out], 0.0)
            value = value + jnp.where(level == levels - 1, sinking * above_in[pl.ds(tracers + m, 1), out], 0.0)
            tang[part, own] = value
            tangent_out[m, :, out] = value

    def adjoint(lo, hi):
        width = (hi - lo) * LANES
        own = pl.ds(LANES + lo * LANES, width)
        out = pl.ds(lo * LANES, width)
        around = pl.ds(lo * LANES, width + 2 * LANES)
        courant, rising, sinking = coef[pl.ds(0, 1), own], coef[pl.ds(2, 1), own], coef[pl.ds(3, 1), own]
        wide_courant, wide_offset = coef[pl.ds(0, 1), around], coef[pl.ds(1, 1), around]
        level = level_rows(width)
        pieces = []
        for m in range(tracers):
            part = pl.ds(m * levels, levels)
            wide = tang[part, around]
            here = wide[:, LANES : LANES + width]
            arrived = jnp.zeros_like(here)
            for shift in range(-HALO, HALO + 1):
                term = jnp.where(wide_offset == float(shift), wide_courant, 0.0) * wide
                if shift != 0:
                    term = pltpu.roll(term, shift % (width + 2 * LANES), 1)
                arrived = arrived + term[:, LANES : LANES + width]
            own_delta = delta[part, own]
            under = below_in[pl.ds(m, 1), out] + sinking * own_delta[0:1]
            over = above_in[pl.ds(m, 1), out] + rising * own_delta[levels - 1 : levels]
            under = jnp.where(lev > 0, under, 0.0)
            over = jnp.where(lev < n_lev - 1, over, 0.0)
            lower = jnp.where(level == 0, under, pltpu.roll(here, 1, 0))
            upper = jnp.where(level == levels - 1, over, pltpu.roll(here, levels - 1, 0))
            diagonal = 1.0 - courant - rising - sinking - loss[part, out]
            pieces.append(diagonal * here + arrived + rising * upper + sinking * lower)
        value = jnp.concatenate(pieces, axis=0).astype(jnp.bfloat16)
        adj[:, out] = value
        if lo == 0:
            adj[:, pl.ds(cols, span)] = value[:, :span]

    for d in range(reach):
        place_weight(d)
    for d in (0, 7, 6):
        forward[d].wait_recv()
    finish_block(0)
    finish_block(7)
    for copy in delta_edges:
        copy.start()
    for copy in (*delta_edges, *coef_edges):
        copy.wait_recv()
    for lo, hi in stage_ranges[0]:
        tangent_partial(lo, hi)
    level_start(0)
    for d in (1, 5, 2):
        forward[d].wait_recv()
    for b in (1, 6, 2, 5):
        finish_block(b)
    for lo, hi in stage_ranges[1]:
        tangent_partial(lo, hi)
    level_start(1)
    level_wait(0)
    for lo, hi in stage_ranges[0]:
        tangent_finish(lo, hi)
    for copy in tang_edges:
        copy.start()
    forward[3].wait_recv()
    for b in (3, 4):
        finish_block(b)
    for lo, hi in stage_ranges[2]:
        tangent_partial(lo, hi)
    level_start(2)
    level_wait(1)
    for lo, hi in stage_ranges[1]:
        tangent_finish(lo, hi)
    for copy in tang_edges:
        copy.wait_recv()
    adjoint(0, 4)
    adjoint(12, tiles)
    for d in (0, 7, 6):
        giving[d].start()
    level_wait(2)
    for lo, hi in stage_ranges[2]:
        tangent_finish(lo, hi)
    adjoint(4, 12)
    for d in (1, 2, 5, 3):
        giving[d].start()

    for d in (centre, 0, 7, 6, 1, 2, 5, 3):
        if d == centre:
            returned = adj[:, pl.ds(d * span, win)]
        else:
            giving[d].wait_recv()
            returned = back[d]
        grad = jnp.dot(returned, shifted[d], preferred_element_type=jnp.float32)
        for t in range(parts + 1):
            placed[d, t + 1] = grad[:, t * LANES : (t + 1) * LANES]

    last = placed.shape[1] - 1
    for t in range(tiles):
        value = None
        for d in range(reach):
            at = lax.min(lax.max(t + 1 - firsts[d], 0), last)
            piece = placed[d, at]
            value = piece if value is None else value + piece
        for m in range(tracers):
            grad_out[m, :, pl.ds(t * LANES, LANES)] = value[m * levels : (m + 1) * levels]

    for copy in (*forward.values(), *giving.values(), *coef_edges, *delta_edges, *tang_edges):
        copy.wait_send()

    @pl.when(lev < n_lev - 1)
    def _():
        for copy in level_up.values():
            copy.wait_send()

    @pl.when(lev > 0)
    def _():
        for copy in level_down.values():
            copy.wait_send()


def shards(n_tile, n_lev, trajectory, increment, counts, remap_weight, kappa, courant, vertical, offset):
    tracers, levels, cols = trajectory.shape
    reach, win, cap = remap_weight.shape[1:]
    rows = tracers * levels
    span = cols // reach
    wide = cols + 2 * LANES
    f32, bf16 = jnp.float32, jnp.bfloat16
    vmem = pl.BlockSpec(memory_space=pltpu.VMEM)
    smem = pl.BlockSpec(memory_space=pltpu.SMEM)
    dma = pltpu.SemaphoreType.DMA
    out = jax.ShapeDtypeStruct((tracers, levels, cols), f32)
    return pl.pallas_call(
        functools.partial(kernel, n_tile, n_lev),
        out_shape=(out, out),
        in_specs=[vmem, vmem, smem, smem, vmem, vmem, vmem, pl.BlockSpec(memory_space=pl.ANY)],
        out_specs=(vmem, vmem),
        scratch_shapes=[
            pltpu.VMEM((reach, win, cap), bf16),
            pltpu.VMEM((reach, win, cap + LANES), bf16),
            pltpu.VMEM((cols // LANES + cap // LANES + 1, 2 * rows, LANES), bf16),
            pltpu.VMEM((reach, 2 * rows, win), f32),
            pltpu.VMEM((reach, 2 * rows, win), f32),
            pltpu.VMEM((8, wide), f32),
            pltpu.VMEM((rows, wide), f32),
            pltpu.VMEM((rows, cols), f32),
            pltpu.VMEM((rows, wide), f32),
            pltpu.VMEM((8, cols), f32),
            pltpu.VMEM((8, cols), f32),
            pltpu.VMEM((8, cols), f32),
            pltpu.VMEM((8, cols), f32),
            pltpu.VMEM((rows, cols + span), bf16),
            pltpu.VMEM((reach, rows, win), bf16),
            pltpu.VMEM((reach, cap // LANES + 3, rows, LANES), f32),
            dma((reach,)),
            dma((reach,)),
            dma((reach,)),
            dma((2,)),
            dma((2,)),
            dma((4,)),
            dma((4,)),
            dma((10,)),
            dma((10,)),
            dma((reach,)),
            dma((reach,)),
        ],
        compiler_params=pltpu.CompilerParams(
            collective_id=0, has_side_effects=True, vmem_limit_bytes=60 * 1024 * 1024
        ),
    )(
        trajectory,
        increment,
        counts,
        kappa,
        courant.reshape(1, cols),
        vertical.reshape(1, cols),
        offset.reshape(1, cols),
        remap_weight,
    )


def solution(mesh):
    return jax.shard_map(
        functools.partial(shards, mesh.shape["tile"], mesh.shape["lev"]),
        mesh=mesh,
        in_specs=(
            P(None, "lev", "tile"),
            P(None, "lev", "tile"),
            P("tile", None),
            P("tile", None, None, None),
            P(),
            P("tile"),
            P("tile"),
            P("tile"),
        ),
        out_specs=(P(None, "lev", "tile"), P(None, "lev", "tile")),
        check_vma=False,
    )
```

time: 157 us -> 44.8 us (0.29); the launches traced: 155 us -> 44.6 us
  starting transfers between devices: 78.6 us -> 0 us
  Pallas kernels: 0 us -> 40.7 us
  other arithmetic: 29.4 us -> 0 us
  local copies, waits for them, and re-layouts: 23.4 us -> 3.23 us
  waiting for transfers between devices: 16 us -> 0 us
  matrix products: 6.36 us -> 0 us
    ppermute x22 -> x0, starting transfers between devices: 78.6 us -> none  [the longest x14 52.9 us: from_behind(): return lax.ppermute(block, axis, route)]
    pallas_call x0 -> x1, Pallas kernels: none -> 40.7 us  [shards(): pl.pallas_call(functools.partial(kernel, n_tile, n_lev), out_shape=(out,...]
    gather x9 -> x0, local copies, waits for them, and re-layouts: 21.6 us -> none  [the longest x2 12.5 us: shards(): jnp.take(fields, slot_index.reshape(-1), axis=1)]
    select_n x6 -> x0, other arithmetic: 20.3 us -> none  [the longest x4 19.6 us: column_slots(): owner = jnp.searchsorted(group_end, columns, side='right')]
    ppermute x22 -> x0, waiting for transfers between devices: 16 us -> none  [the longest x14 14.6 us: from_behind(): return lax.ppermute(block, axis, route)]
    dot_general x2 -> x0, matrix products: 6.36 us -> none  [the longest x1 3.51 us: shards(): jnp.einsum('fdc,dwc->dfw', slotted, weights, preferred_element_type=jnp.f...]
    and x1 -> x0, other arithmetic: 4.91 us -> none  [shards(): grad_outer = jnp.take(slot_grad.reshape(field_rows, -1), back_index, axis=1)]
    unnamed x25 -> x2, local copies, waits for them, and re-layouts: 0.22 us -> 3.23 us
  transfers between devices with their start and end apart: 22 -> 0, of which waited for: 7 -> 0; matrix products, arithmetic and copies ran while one was open for 18% -> 0% of each run, Pallas kernels for 0% -> 0%
where the time goes in v1:
time: 44.8 us; the launch traced here: 44.6 us
  Pallas kernels  40.7 us (91%)
  local copies, waits for them, and re-layouts  3.23 us (7%)
  between operations  0.64 us (1%)
    pallas_call x1, Pallas kernels, shards(): pl.pallas_call(functools.partial(kernel, n_tile, n_lev), out_shape=(out,...  40.7 us
    unnamed x2, local copies, waits for them, and re-layouts  3.23 us

profile of v1, /device:TPU:1, one launch (start us, length us, event | category | flops | bytes accessed | tf_op | source)
XLA Modules:
  0.0 44.6 jit_solution(16889579255546052616)
XLA Ops:
  0.6 40.7 %shard_map.95 = (f32[3,8,2048]{2,1,0:T(8,128)}, f32[3,8,2048]{2,1,0:T(8,128)}) custom-call(bf16[3,8,2048]{2,1,0:T(8,128)(2,1)} %traj_ref.1, bf16[3,8,2048]{2,1,0:T(8,128)(2,1)} %inc_ref.1, s32[1,8]{1,0:T(1,128)} %counts_ref.1, f32[3]{0:T(128)} %kappa_ref.1, f32[1,2048]{1,0:T(1,128)} %bitcast.3, f32[1,2048]{1,0:T(1,128)} %bitcast.4, s32[1,2048]{1,0:T(1,128)} %bitcast.5, ...), custom_call_target="tpu_custom_call" | custom-call | tf_op jit(solution)/shard_map/pallas_call | solution.py:461
  41.4 1.6 %copy.12 = f32[3,8,2048]{2,1,0:T(8,128)} copy(f32[3,8,2048]{2,1,0:T(8,128)} %get-tuple-element.4) | data formatting | bytes 393216
  43.0 1.6 %copy.13 = f32[3,8,2048]{2,1,0:T(8,128)} copy(f32[3,8,2048]{2,1,0:T(8,128)} %get-tuple-element.5) | data formatting | bytes 393216

commit v2 on v1

--- a/solution.py
+++ b/solution.py
@@ -16,6 +16,16 @@
 def kernel(
     n_tile,
     n_lev,
+    traj_hbm,
+    inc_hbm,
+    counts_hbm,
+    kappa_hbm,
+    courant_hbm,
+    vertical_hbm,
+    offset_hbm,
+    weight_hbm,
+    tangent_out,
+    grad_out,
     traj_ref,
     inc_ref,
     counts_ref,
@@ -23,9 +33,6 @@
     courant_ref,
     vertical_ref,
     offset_ref,
-    weight_hbm,
-    tangent_out,
-    grad_out,
     weight,
     shifted,
     fields,
@@ -42,6 +49,7 @@
     adj,
     back,
     placed,
+    load_sem,
     weight_sem,
     fwd_send,
     fwd_recv,
@@ -54,7 +62,7 @@
     ret_send,
     ret_recv,
 ):
-    tracers, levels, cols = traj_ref.shape
+    tracers, levels, cols = traj_hbm.shape
     rows = tracers * levels
     reach = weight_hbm.shape[1]
     win, cap = weight_hbm.shape[2], weight_hbm.shape[3]
@@ -68,12 +76,6 @@
     def tile_at(distance):
         return (lax.rem(me + (n_tile + distance), n_tile), lev)
 
-    weight_copies = [
-        pltpu.make_async_copy(weight_hbm.at[0, d], weight.at[d], weight_sem.at[d]) for d in range(reach)
-    ]
-    for d in SEND_ORDER:
-        weight_copies[d].start()
-
     barrier = pltpu.get_barrier_semaphore()
     for distance in range(-centre, centre + 1):
         if distance != 0:
@@ -87,6 +89,30 @@
     def _():
         pl.semaphore_signal(barrier, inc=1, device_id=(me, lev + 1), device_id_type=MESH)
 
+    loads = [
+        pltpu.make_async_copy(source, target, load_sem.at[i])
+        for i, (source, target) in enumerate(
+            (
+                (counts_hbm, counts_ref),
+                (kappa_hbm, kappa_ref),
+                (traj_hbm, traj_ref),
+                (inc_hbm, inc_ref),
+                (courant_hbm, courant_ref),
+                (vertical_hbm, vertical_ref),
+                (offset_hbm, offset_ref),
+            )
+        )
+    ]
+    weight_copies = [
+        pltpu.make_async_copy(weight_hbm.at[0, d], weight.at[d], weight_sem.at[d]) for d in range(reach)
+    ]
+    for copy in loads:
+        copy.start()
+    for d in SEND_ORDER:
+        weight_copies[d].start()
+
+    for copy in loads:
+        copy.wait()
     stacked = jnp.concatenate(
         [ref[m].astype(jnp.float32) for ref in (traj_ref, inc_ref) for m in range(tracers)], axis=0
     ).astype(jnp.bfloat16)
@@ -455,15 +481,21 @@
     wide = cols + 2 * LANES
     f32, bf16 = jnp.float32, jnp.bfloat16
     vmem = pl.BlockSpec(memory_space=pltpu.VMEM)
-    smem = pl.BlockSpec(memory_space=pltpu.SMEM)
     dma = pltpu.SemaphoreType.DMA
     out = jax.ShapeDtypeStruct((tracers, levels, cols), f32)
     return pl.pallas_call(
         functools.partial(kernel, n_tile, n_lev),
         out_shape=(out, out),
-        in_specs=[vmem, vmem, smem, smem, vmem, vmem, vmem, pl.BlockSpec(memory_space=pl.ANY)],
+        in_specs=[pl.BlockSpec(memory_space=pltpu.HBM)] * 8,
         out_specs=(vmem, vmem),
         scratch_shapes=[
+            pltpu.VMEM((tracers, levels, cols), bf16),
+            pltpu.VMEM((tracers, levels, cols), bf16),
+            pltpu.SMEM((1, reach), jnp.int32),
+            pltpu.SMEM((tracers,), f32),
+            pltpu.VMEM((1, cols), f32),
+            pltpu.VMEM((1, cols), f32),
+            pltpu.VMEM((1, cols), jnp.int32),
             pltpu.VMEM((reach, win, cap), bf16),
             pltpu.VMEM((reach, win, cap + LANES), bf16),
             pltpu.VMEM((cols // LANES + cap // LANES + 1, 2 * rows, LANES), bf16),
@@ -480,6 +512,7 @@
             pltpu.VMEM((rows, cols + span), bf16),
             pltpu.VMEM((reach, rows, win), bf16),
             pltpu.VMEM((reach, cap // LANES + 3, rows, LANES), f32),
+            dma((7,)),
             dma((reach,)),
             dma((reach,)),
             dma((reach,)),
@@ -493,17 +526,22 @@
             dma((reach,)),
         ],
         compiler_params=pltpu.CompilerParams(
-            collective_id=0, has_side_effects=True, vmem_limit_bytes=60 * 1024 * 1024
+            collective_id=0, has_side_effects=True, vmem_limit_bytes=24 * 1024 * 1024
         ),
     )(
-        trajectory,
-        increment,
-        counts,
-        kappa,
-        courant.reshape(1, cols),
-        vertical.reshape(1, cols),
-        offset.reshape(1, cols),
-        remap_weight,
+        *(
+            pltpu.with_memory_space_constraint(operand, pltpu.HBM)
+            for operand in (
+                trajectory,
+                increment,
+                counts,
+                kappa,
+                courant.reshape(1, cols),
+                vertical.reshape(1, cols),
+                offset.reshape(1, cols),
+                remap_weight,
+            )
+        )
     )
 
 

time: 44.8 us -> 41.3 us (0.922)
  local copies, waits for them, and re-layouts: 3.23 us -> 1.36 us
  Pallas kernels: 40.7 us -> 39.2 us
    unnamed x2, local copies, waits for them, and re-layouts: 3.23 us -> 1.36 us
    pallas_call x1, Pallas kernels: 40.7 us -> 39.2 us  [shards(): pl.pallas_call(functools.partial(kernel, n_tile, n_lev), out_shape=(out,...]
where the time goes in v2:
time: 41.3 us; the launch traced here: 41.2 us
  Pallas kernels  39.2 us (95%)
  local copies, waits for them, and re-layouts  1.36 us (3%)
  between operations  0.64 us (2%)
    pallas_call x1, Pallas kernels, shards(): pl.pallas_call(functools.partial(kernel, n_tile, n_lev), out_shape=(out,...  39.2 us
    unnamed x2, local copies, waits for them, and re-layouts  1.36 us

profile of v2, /device:TPU:1, one launch (start us, length us, event | category | flops | bytes accessed | tf_op | source)
XLA Modules:
  0.0 41.2 jit_solution(8261780469908253720)
XLA Ops:
  0.6 39.2 %shard_map.95 = (f32[3,8,2048]{2,1,0:T(8,128)S(1)}, f32[3,8,2048]{2,1,0:T(8,128)S(1)}) custom-call(bf16[3,8,2048]{2,1,0:T(8,128)(2,1)} %traj_hbm.1, bf16[3,8,2048]{2,1,0:T(8,128)(2,1)} %inc_hbm.1, s32[1,8]{1,0:T(1,128)} %counts_hbm.1, f32[3]{0:T(128)} %kappa_hbm.1, f32[1,2048]{1,0:T(1,128)} %bitcast.3, f32[1,2048]{1,0:T(1,128)} %bitcast.4, ...), custom_call_target="tpu_custom_call" | custom-call | tf_op jit(solution)/shard_map/pallas_call | solution.py:486
  39.8 0.7 %copy.12 = f32[3,8,2048]{2,1,0:T(8,128)} copy(f32[3,8,2048]{2,1,0:T(8,128)S(1)} %get-tuple-element.4) | data formatting | bytes 393216
  40.5 0.7 %copy.13 = f32[3,8,2048]{2,1,0:T(8,128)} copy(f32[3,8,2048]{2,1,0:T(8,128)S(1)} %get-tuple-element.5) | data formatting | bytes 393216

commit v3 on v2

--- a/solution.py
+++ b/solution.py
@@ -10,7 +10,9 @@
 MESH = pl.DeviceIdType.MESH
 LANES = 128
 HALO = 2
-SEND_ORDER = (0, 7, 1, 6, 2, 5, 3, 4)
+SEND_ORDER = (0, 7, 6, 1, 2, 3, 5, 4)
+EVEN, ODD = (0,), (1,)
+BOTH = (0, 1)
 
 
 def kernel(
@@ -37,6 +39,8 @@
     shifted,
     fields,
     outgoing,
+    mixing,
+    summed,
     recv,
     coef,
     delta,
@@ -46,6 +50,11 @@
     down_out,
     below_in,
     above_in,
+    edge_up,
+    edge_down,
+    edge_below,
+    edge_above,
+    edge_tang,
     adj,
     back,
     placed,
@@ -126,16 +135,18 @@
     coef[pl.ds(2, 1), pl.ds(LANES, cols)] = jnp.maximum(vertical, 0.0)
     coef[pl.ds(3, 1), pl.ds(LANES, cols)] = jnp.maximum(-vertical, 0.0)
     coef[pl.ds(4, 4), pl.ds(LANES, cols)] = jnp.zeros((4, cols), jnp.float32)
-    up_out[pl.ds(6, 2), :] = jnp.zeros((2, cols), jnp.float32)
-    down_out[pl.ds(6, 2), :] = jnp.zeros((2, cols), jnp.float32)
+    for ref in (up_out, down_out, edge_up, edge_down):
+        ref[pl.ds(6, 2), :] = jnp.zeros((2, ref.shape[1]), jnp.float32)
 
     @pl.when(lev == 0)
     def _():
         below_in[...] = jnp.zeros_like(below_in)
+        edge_below[...] = jnp.zeros_like(edge_below)
 
     @pl.when(lev == n_lev - 1)
     def _():
         above_in[...] = jnp.zeros_like(above_in)
+        edge_above[...] = jnp.zeros_like(edge_above)
 
     placed[:, pl.ds(0, 1)] = jnp.zeros((reach, 1, rows, LANES), jnp.float32)
     placed[:, pl.ds(placed.shape[1] - 1, 1)] = jnp.zeros((reach, 1, rows, LANES), jnp.float32)
@@ -185,18 +196,68 @@
             )
             shifted[d, :, pl.ds(t * LANES, LANES)] = moved.astype(jnp.bfloat16)
 
+    parity = lax.rem(me, 2)
+    half = win // 2
+
+    def on_core(cores, run):
+        if len(cores) == 2:
+            run()
+        else:
+            pl.when(parity == cores[0])(run)
+
+    def window_part(d, lane, width):
+        part = pl.ds(lane, width)
+        return outgoing.at[d, :, part], recv.at[d, :, part], d - centre
+
+    plan = {
+        "e0": (BOTH, *window_part(0, 0, LANES)),
+        "e7": (BOTH, *window_part(7, LANES, 2 * LANES)),
+        "e6": (BOTH, *window_part(6, 3 * LANES, LANES)),
+        "g0w": (EVEN, *window_part(0, LANES, 3 * LANES)),
+        "g0l": (ODD, *window_part(0, LANES, LANES)),
+        "g7z": (BOTH, *window_part(7, 3 * LANES, LANES)),
+        "g7a": (ODD, *window_part(7, 0, LANES)),
+        "g6m": (EVEN, *window_part(6, half, LANES)),
+        "g6l": (ODD, *window_part(6, 0, half)),
+        "g1h": (EVEN, *window_part(1, half, half)),
+        "g1l": (ODD, *window_part(1, 0, half)),
+        "g2h": (EVEN, *window_part(2, half, half)),
+        "g2l": (ODD, *window_part(2, 0, half)),
+        "g3h": (EVEN, *window_part(3, half, half)),
+        "g3w": (ODD, *window_part(3, 0, win)),
+        "g5w": (EVEN, *window_part(5, 0, win)),
+        "g5l": (ODD, *window_part(5, 0, half)),
+        "m1": (EVEN, outgoing.at[1, :, pl.ds(0, half)], mixing.at[0], 1),
+        "m2": (EVEN, outgoing.at[2, :, pl.ds(0, half)], mixing.at[1], 1),
+        "m3": (EVEN, outgoing.at[3, :, pl.ds(0, half)], mixing.at[2], 1),
+        "m5": (ODD, outgoing.at[5, :, pl.ds(half, half)], mixing.at[0], -1),
+        "m6": (ODD, outgoing.at[6, :, pl.ds(half, LANES)], mixing.at[1, :, pl.ds(0, LANES)], -1),
+        "c1": (ODD, summed.at[0], recv.at[1, :, pl.ds(0, half)], -4),
+        "c2": (ODD, summed.at[1], recv.at[2, :, pl.ds(0, half)], -3),
+        "c3": (ODD, summed.at[2], recv.at[3, :, pl.ds(0, half)], -2),
+        "c6": (EVEN, summed.at[0], recv.at[6, :, pl.ds(0, half)], 2),
+        "c7": (EVEN, summed.at[1, :, pl.ds(0, LANES)], recv.at[7, :, pl.ds(0, LANES)], 3),
+    }
     forward = {
-        d: pltpu.make_async_remote_copy(
-            src_ref=outgoing.at[d],
-            dst_ref=recv.at[d],
-            send_sem=fwd_send.at[d],
-            recv_sem=fwd_recv.at[d],
-            device_id=tile_at(d - centre),
+        name: pltpu.make_async_remote_copy(
+            src_ref=source,
+            dst_ref=target,
+            send_sem=fwd_send.at[i],
+            recv_sem=fwd_recv.at[i],
+            device_id=tile_at(distance),
             device_id_type=MESH,
         )
-        for d in range(reach)
-        if d != centre
+        for i, (name, (_, source, target, distance)) in enumerate(plan.items())
     }
+
+    def send(*names):
+        for name in names:
+            on_core(plan[name][0], forward[name].start)
+
+    def arrived(*names):
+        for name in names:
+            forward[name].wait_recv()
+
     giving = {
         d: pltpu.make_async_remote_copy(
             src_ref=adj.at[:, pl.ds(d * span, win)],
@@ -210,9 +271,9 @@
         if d != centre
     }
 
-    def edges(ref, send_sem, recv_sem, base):
+    def edges(first, last, ref, send_sem, recv_sem, base):
         left = pltpu.make_async_remote_copy(
-            src_ref=ref.at[:, pl.ds(LANES, LANES)],
+            src_ref=first,
             dst_ref=ref.at[:, pl.ds(LANES + cols, LANES)],
             send_sem=send_sem.at[base],
             recv_sem=recv_sem.at[base],
@@ -220,7 +281,7 @@
             device_id_type=MESH,
         )
         right = pltpu.make_async_remote_copy(
-            src_ref=ref.at[:, pl.ds(cols, LANES)],
+            src_ref=last,
             dst_ref=ref.at[:, pl.ds(0, LANES)],
             send_sem=send_sem.at[base + 1],
             recv_sem=recv_sem.at[base + 1],
@@ -229,60 +290,79 @@
         )
         return left, right
 
-    coef_edges = edges(coef, coef_send, coef_recv, 0)
-    delta_edges = edges(delta, col_send, col_recv, 0)
-    tang_edges = edges(tang, col_send, col_recv, 2)
-
-    stage_ranges = (
-        ((0, 1), (tiles - 1, tiles)),
-        ((1, 5), (11, tiles - 1)),
-        ((5, 11),),
+    first_tile, last_tile = pl.ds(LANES, LANES), pl.ds(cols, LANES)
+    coef_edges = edges(coef.at[:, first_tile], coef.at[:, last_tile], coef, coef_send, coef_recv, 0)
+    delta_edges = edges(delta.at[:, first_tile], delta.at[:, last_tile], delta, col_send, col_recv, 0)
+    tang_edges = edges(
+        edge_tang.at[:, pl.ds(LANES, LANES)], edge_tang.at[:, pl.ds(0, LANES)], tang, col_send, col_recv, 2
     )
-    level_up, level_down = {}, {}
+
+    early = ((0, 5), (11, tiles))
+    late = ((5, 11),)
+    everything = ((0, 2),)
+    stages = (
+        (everything, edge_up, edge_down, edge_below, edge_above),
+        (early, up_out, down_out, below_in, above_in),
+        (late, up_out, down_out, below_in, above_in),
+    )
+    level_up, level_down = ([], [], []), ([], [], [])
     index = 0
-    for ranges in stage_ranges:
+    for stage, (ranges, up_from, down_from, up_to, down_to) in enumerate(stages):
         for lo, hi in ranges:
             part = pl.ds(lo * LANES, (hi - lo) * LANES)
-            level_up[lo, hi] = pltpu.make_async_remote_copy(
-                src_ref=up_out.at[:, part],
-                dst_ref=below_in.at[:, part],
-                send_sem=lev_send.at[index],
-                recv_sem=lev_recv.at[index],
-                device_id=(me, lax.rem(lev + 1, n_lev)),
-                device_id_type=MESH,
+            level_up[stage].append(
+                pltpu.make_async_remote_copy(
+                    src_ref=up_from.at[:, part],
+                    dst_ref=up_to.at[:, part],
+                    send_sem=lev_send.at[index],
+                    recv_sem=lev_recv.at[index],
+                    device_id=(me, lax.rem(lev + 1, n_lev)),
+                    device_id_type=MESH,
+                )
             )
-            level_down[lo, hi] = pltpu.make_async_remote_copy(
-                src_ref=down_out.at[:, part],
-                dst_ref=above_in.at[:, part],
-                send_sem=lev_send.at[index + 1],
-                recv_sem=lev_recv.at[index + 1],
-                device_id=(me, lax.rem(lev + n_lev - 1, n_lev)),
-                device_id_type=MESH,
+            level_down[stage].append(
+                pltpu.make_async_remote_copy(
+                    src_ref=down_from.at[:, part],
+                    dst_ref=down_to.at[:, part],
+                    send_sem=lev_send.at[index + 1],
+                    recv_sem=lev_recv.at[index + 1],
+                    device_id=(me, lax.rem(lev + n_lev - 1, n_lev)),
+                    device_id_type=MESH,
+                )
             )
             index += 2
 
     def level_start(stage):
         @pl.when(lev < n_lev - 1)
         def _():
-            for key in stage_ranges[stage]:
-                level_up[key].start()
+            for copy in level_up[stage]:
+                copy.start()
 
         @pl.when(lev > 0)
         def _():
-            for key in stage_ranges[stage]:
-                level_down[key].start()
+            for copy in level_down[stage]:
+                copy.start()
 
     def level_wait(stage):
         @pl.when(lev > 0)
         def _():
-            for key in stage_ranges[stage]:
-                level_up[key].wait_recv()
+            for copy in level_up[stage]:
+                copy.wait_recv()
 
         @pl.when(lev < n_lev - 1)
         def _():
-            for key in stage_ranges[stage]:
-                level_down[key].wait_recv()
-
+            for copy in level_down[stage]:
+                copy.wait_recv()
+
+    sends = {
+        0: ("e0", "g0w", "g0l"),
+        7: ("e7",),
+        6: ("e6", "m6", "g7z", "g7a", "g6m", "g6l"),
+        1: ("m1", "g1h", "g1l"),
+        2: ("m2", "g2h", "g2l"),
+        3: ("m3", "g3h", "g3w"),
+        5: ("m5", "g5w", "g5l"),
+    }
     for position, d in enumerate(SEND_ORDER):
         slotted = slots_of(d)
         weight_copies[d].wait()
@@ -298,22 +378,42 @@
                     barrier,
                     2 * centre + (lev > 0).astype(jnp.int32) + (lev < n_lev - 1).astype(jnp.int32),
                 )
-            forward[d].start()
+            send(*sends[d])
             if position == 0:
                 for copy in coef_edges:
                     copy.start()
 
-    def finish_block(b):
-        value = recv[b, :, pl.ds(0, span)] + recv[(b - 1) % reach, :, pl.ds(span, span)]
+    @pl.when(parity == 1)
+    def _():
+        for b in (1, 2, 3):
+            arrived(f"m{b}")
+            summed[b - 1] = outgoing[b - 1, :, pl.ds(half, half)] + mixing[b - 1]
+            forward[f"c{b}"].start()
+
+    @pl.when(parity == 0)
+    def _():
+        arrived("m6")
+        part = pl.ds(0, LANES)
+        summed[1, :, part] = outgoing[7, :, part] + mixing[1, :, part]
+        forward["c7"].start()
+        arrived("m5")
+        summed[0] = outgoing[6, :, pl.ds(0, half)] + mixing[0]
+        forward["c6"].start()
+
+    def finish(column, width, *pieces):
+        value = None
+        for d, at in pieces:
+            piece = recv[d, :, pl.ds(at, width)]
+            value = piece if value is None else value + piece
         for m in range(tracers):
             part = pl.ds(m * levels, levels)
-            loss[part, pl.ds(b * span, span)] = 2.0 * kappa_ref[m] * value[m * levels : (m + 1) * levels]
-        delta[:, pl.ds(LANES + b * span, span)] = value[rows:]
+            loss[part, pl.ds(column, width)] = 2.0 * kappa_ref[m] * value[m * levels : (m + 1) * levels]
+        delta[:, pl.ds(LANES + column, width)] = value[rows:]
 
     def level_rows(width):
         return lax.broadcasted_iota(jnp.int32, (levels, width), 0)
 
-    def tangent_partial(lo, hi):
+    def tangent_partial(lo, hi, tang_to, at, up_to, down_to, out_at):
         width = (hi - lo) * LANES
         own = pl.ds(LANES + lo * LANES, width)
         courant, offset = coef[pl.ds(0, 1), own], coef[pl.ds(1, 1), own]
@@ -338,26 +438,32 @@
                 + sinking * (above - here)
                 - loss[part, pl.ds(lo * LANES, width)] * here
             )
-            tang[part, own] = value
-            out = pl.ds(lo * LANES, width)
-            up_out[pl.ds(m, 1), out] = value[levels - 1 : levels]
-            up_out[pl.ds(tracers + m, 1), out] = here[levels - 1 : levels]
-            down_out[pl.ds(m, 1), out] = value[0:1]
-            down_out[pl.ds(tracers + m, 1), out] = here[0:1]
+            tang_to[part, pl.ds(at, width)] = value
+            out = pl.ds(out_at, width)
+            up_to[pl.ds(m, 1), out] = value[levels - 1 : levels]
+            up_to[pl.ds(tracers + m, 1), out] = here[levels - 1 : levels]
+            down_to[pl.ds(m, 1), out] = value[0:1]
+            down_to[pl.ds(tracers + m, 1), out] = here[0:1]
+
+    def level_terms(value, m, width, rising, sinking, below, above, out):
+        level = level_rows(width)
+        value = value + jnp.where(level == 0, rising * below[pl.ds(tracers + m, 1), out], 0.0)
+        return value + jnp.where(level == levels - 1, sinking * above[pl.ds(tracers + m, 1), out], 0.0)
 
     def tangent_finish(lo, hi):
         width = (hi - lo) * LANES
         own = pl.ds(LANES + lo * LANES, width)
         out = pl.ds(lo * LANES, width)
         rising, sinking = coef[pl.ds(2, 1), own], coef[pl.ds(3, 1), own]
-        level = level_rows(width)
         for m in range(tracers):
             part = pl.ds(m * levels, levels)
-            value = tang[part, own]
-            value = value + jnp.where(level == 0, rising * below_in[pl.ds(tracers + m, 1), out], 0.0)
-            value = value + jnp.where(level == levels - 1, sinking * above_in[pl.ds(tracers + m, 1), out], 0.0)
+            value = level_terms(tang[part, own], m, width, rising, sinking, below_in, above_in, out)
             tang[part, own] = value
             tangent_out[m, :, out] = value
+
+    def main_partial(ranges):
+        for lo, hi in ranges:
+            tangent_partial(lo, hi, tang, LANES + lo * LANES, up_out, down_out, lo * LANES)
 
     def adjoint(lo, hi):
         width = (hi - lo) * LANES
@@ -372,12 +478,12 @@
             part = pl.ds(m * levels, levels)
             wide = tang[part, around]
             here = wide[:, LANES : LANES + width]
-            arrived = jnp.zeros_like(here)
+            total = jnp.zeros_like(here)
             for shift in range(-HALO, HALO + 1):
                 term = jnp.where(wide_offset == float(shift), wide_courant, 0.0) * wide
                 if shift != 0:
                     term = pltpu.roll(term, shift % (width + 2 * LANES), 1)
-                arrived = arrived + term[:, LANES : LANES + width]
+                total = total + term[:, LANES : LANES + width]
             own_delta = delta[part, own]
             under = below_in[pl.ds(m, 1), out] + sinking * own_delta[0:1]
             over = above_in[pl.ds(m, 1), out] + rising * own_delta[levels - 1 : levels]
@@ -386,45 +492,82 @@
             lower = jnp.where(level == 0, under, pltpu.roll(here, 1, 0))
             upper = jnp.where(level == levels - 1, over, pltpu.roll(here, levels - 1, 0))
             diagonal = 1.0 - courant - rising - sinking - loss[part, out]
-            pieces.append(diagonal * here + arrived + rising * upper + sinking * lower)
+            pieces.append(diagonal * here + total + rising * upper + sinking * lower)
         value = jnp.concatenate(pieces, axis=0).astype(jnp.bfloat16)
         adj[:, out] = value
         if lo == 0:
             adj[:, pl.ds(cols, span)] = value[:, :span]
 
-    for d in range(reach):
-        place_weight(d)
-    for d in (0, 7, 6):
-        forward[d].wait_recv()
-    finish_block(0)
-    finish_block(7)
+    last = cols - LANES
+    arrived("e0", "e7", "e6")
+    finish(0, LANES, (0, 0), (7, half))
+    finish(last, LANES, (7, LANES), (6, 3 * LANES))
     for copy in delta_edges:
         copy.start()
+    for d in (0, 7, 6):
+        place_weight(d)
     for copy in (*delta_edges, *coef_edges):
         copy.wait_recv()
-    for lo, hi in stage_ranges[0]:
-        tangent_partial(lo, hi)
+    tangent_partial(tiles - 1, tiles, edge_tang, 0, edge_up, edge_down, 0)
+    tangent_partial(0, 1, edge_tang, LANES, edge_up, edge_down, LANES)
     level_start(0)
-    for d in (1, 5, 2):
-        forward[d].wait_recv()
-    for b in (1, 6, 2, 5):
-        finish_block(b)
-    for lo, hi in stage_ranges[1]:
-        tangent_partial(lo, hi)
-    level_start(1)
+    for d in (1, 2, 3):
+        place_weight(d)
     level_wait(0)
-    for lo, hi in stage_ranges[0]:
-        tangent_finish(lo, hi)
+    for at, tile in ((0, tiles - 1), (LANES, 0)):
+        own = pl.ds(LANES + tile * LANES, LANES)
+        out = pl.ds(at, LANES)
+        for m in range(tracers):
+            part = pl.ds(m * levels, levels)
+            edge_tang[part, out] = level_terms(
+                edge_tang[part, out], m, LANES, coef[pl.ds(2, 1), own], coef[pl.ds(3, 1), own], edge_below, edge_above, out
+            )
     for copy in tang_edges:
         copy.start()
-    forward[3].wait_recv()
-    for b in (3, 4):
-        finish_block(b)
-    for lo, hi in stage_ranges[2]:
-        tangent_partial(lo, hi)
+    for d in (5, 4):
+        place_weight(d)
+
+    arrived("g7z")
+
+    @pl.when(parity == 0)
+    def _():
+        arrived("g0w", "g7a", "g6m", "g5l", "g1l", "c6", "c2")
+        finish(LANES, LANES, (0, LANES), (7, 3 * LANES))
+        finish(last - LANES, LANES, (7, 0), (6, half))
+        finish(span, span, (1, 0), (0, half))
+        finish(2 * span, span, (2, 0))
+        finish(5 * span, span, (5, 0), (4, half))
+        finish(6 * span, span, (6, 0))
+
+    @pl.when(parity == 1)
+    def _():
+        arrived("g0l", "c7", "g6l", "g5w", "g2l", "g1h", "c1")
+        finish(LANES, LANES, (0, LANES), (7, 3 * LANES))
+        finish(last - LANES, LANES, (7, 0))
+        finish(span, span, (1, 0))
+        finish(2 * span, span, (2, 0), (1, half))
+        finish(5 * span, span, (5, 0), (4, half))
+        finish(6 * span, span, (6, 0), (5, half))
+
+    main_partial(early)
+    level_start(1)
+
+    @pl.when(parity == 0)
+    def _():
+        arrived("g2h", "g3w")
+        finish(3 * span, span, (3, 0), (2, half))
+        finish(4 * span, span, (4, 0), (3, half))
+
+    @pl.when(parity == 1)
+    def _():
+        arrived("c3", "g3h")
+        finish(3 * span, span, (3, 0))
+        finish(4 * span, span, (4, 0), (3, half))
+
+    main_partial(late)
     level_start(2)
     level_wait(1)
-    for lo, hi in stage_ranges[1]:
+    for lo, hi in early:
         tangent_finish(lo, hi)
     for copy in tang_edges:
         copy.wait_recv()
@@ -433,7 +576,7 @@
     for d in (0, 7, 6):
         giving[d].start()
     level_wait(2)
-    for lo, hi in stage_ranges[2]:
+    for lo, hi in late:
         tangent_finish(lo, hi)
     adjoint(4, 12)
     for d in (1, 2, 5, 3):
@@ -449,28 +592,32 @@
         for t in range(parts + 1):
             placed[d, t + 1] = grad[:, t * LANES : (t + 1) * LANES]
 
-    last = placed.shape[1] - 1
+    top = placed.shape[1] - 1
     for t in range(tiles):
         value = None
         for d in range(reach):
-            at = lax.min(lax.max(t + 1 - firsts[d], 0), last)
+            at = lax.min(lax.max(t + 1 - firsts[d], 0), top)
             piece = placed[d, at]
             value = piece if value is None else value + piece
         for m in range(tracers):
             grad_out[m, :, pl.ds(t * LANES, LANES)] = value[m * levels : (m + 1) * levels]
 
-    for copy in (*forward.values(), *giving.values(), *coef_edges, *delta_edges, *tang_edges):
+    for name, copy in forward.items():
+        on_core(plan[name][0], copy.wait_send)
+    for copy in (*giving.values(), *coef_edges, *delta_edges, *tang_edges):
         copy.wait_send()
 
     @pl.when(lev < n_lev - 1)
     def _():
-        for copy in level_up.values():
-            copy.wait_send()
+        for copies in level_up:
+            for copy in copies:
+                copy.wait_send()
 
     @pl.when(lev > 0)
     def _():
-        for copy in level_down.values():
-            copy.wait_send()
+        for copies in level_down:
+            for copy in copies:
+                copy.wait_send()
 
 
 def shards(n_tile, n_lev, trajectory, increment, counts, remap_weight, kappa, courant, vertical, offset):
@@ -500,6 +647,8 @@
             pltpu.VMEM((reach, win, cap + LANES), bf16),
             pltpu.VMEM((cols // LANES + cap // LANES + 1, 2 * rows, LANES), bf16),
             pltpu.VMEM((reach, 2 * rows, win), f32),
+            pltpu.VMEM((3, 2 * rows, win // 2), f32),
+            pltpu.VMEM((3, 2 * rows, win // 2), f32),
             pltpu.VMEM((reach, 2 * rows, win), f32),
             pltpu.VMEM((8, wide), f32),
             pltpu.VMEM((rows, wide), f32),
@@ -509,13 +658,18 @@
             pltpu.VMEM((8, cols), f32),
             pltpu.VMEM((8, cols), f32),
             pltpu.VMEM((8, cols), f32),
+            pltpu.VMEM((8, 2 * LANES), f32),
+            pltpu.VMEM((8, 2 * LANES), f32),
+            pltpu.VMEM((8, 2 * LANES), f32),
+            pltpu.VMEM((8, 2 * LANES), f32),
+            pltpu.VMEM((rows, 2 * LANES), f32),
             pltpu.VMEM((rows, cols + span), bf16),
             pltpu.VMEM((reach, rows, win), bf16),
             pltpu.VMEM((reach, cap // LANES + 3, rows, LANES), f32),
             dma((7,)),
             dma((reach,)),
-            dma((reach,)),
-            dma((reach,)),
+            dma((27,)),
+            dma((27,)),
             dma((2,)),
             dma((2,)),
             dma((4,)),

time: 41.3 us -> 40.8 us (0.988)
  Pallas kernels: 39.2 us -> 38.6 us
    pallas_call x1, Pallas kernels: 39.2 us -> 38.6 us  [shards(): pl.pallas_call(functools.partial(kernel, n_tile, n_lev), out_shape=(out,...]
where the time goes in v3:
time: 40.8 us; the launch traced here: 40.6 us
  Pallas kernels  38.6 us (95%)
  local copies, waits for them, and re-layouts  1.36 us (3%)
  between operations  0.64 us (2%)
    pallas_call x1, Pallas kernels, shards(): pl.pallas_call(functools.partial(kernel, n_tile, n_lev), out_shape=(out,...  38.6 us
    unnamed x2, local copies, waits for them, and re-layouts  1.36 us

profile of v3, /device:TPU:1, one launch (start us, length us, event | category | flops | bytes accessed | tf_op | source)
XLA Modules:
  0.0 40.6 jit_solution(4549988861296536294)
XLA Ops:
  0.6 38.6 %shard_map.95 = (f32[3,8,2048]{2,1,0:T(8,128)S(1)}, f32[3,8,2048]{2,1,0:T(8,128)S(1)}) custom-call(bf16[3,8,2048]{2,1,0:T(8,128)(2,1)} %traj_hbm.1, bf16[3,8,2048]{2,1,0:T(8,128)(2,1)} %inc_hbm.1, s32[1,8]{1,0:T(1,128)} %counts_hbm.1, f32[3]{0:T(128)} %kappa_hbm.1, f32[1,2048]{1,0:T(1,128)} %bitcast.3, f32[1,2048]{1,0:T(1,128)} %bitcast.4, ...), custom_call_target="tpu_custom_call" | custom-call | tf_op jit(solution)/shard_map/pallas_call | solution.py:633
  39.3 0.7 %copy.12 = f32[3,8,2048]{2,1,0:T(8,128)} copy(f32[3,8,2048]{2,1,0:T(8,128)S(1)} %get-tuple-element.4) | data formatting | bytes 393216
  40.0 0.7 %copy.13 = f32[3,8,2048]{2,1,0:T(8,128)} copy(f32[3,8,2048]{2,1,0:T(8,128)S(1)} %get-tuple-element.5) | data formatting | bytes 393216

commit v4 on v3

v4 whole, which is shorter than its diff:
```python
import functools

import jax
import jax.numpy as jnp
from jax import lax
from jax.experimental import pallas as pl
from jax.experimental.pallas import tpu as pltpu
from jax.sharding import PartitionSpec as P

MESH = pl.DeviceIdType.MESH
LANES = 128
HALO = 2
FIRST, REST = (0, 7, 6), (1, 2, 3, 5, 4)
EVEN, ODD = (0,), (1,)
BOTH = (0, 1)


def kernel(
    n_tile,
    n_lev,
    traj_hbm,
    inc_hbm,
    counts_hbm,
    kappa_hbm,
    courant_hbm,
    vertical_hbm,
    offset_hbm,
    weight_hbm,
    tangent_out,
    grad_out,
    traj_ref,
    inc_ref,
    counts_ref,
    kappa_ref,
    courant_ref,
    vertical_ref,
    offset_ref,
    weight,
    shifted,
    fields,
    outgoing,
    mixing,
    summed,
    recv,
    coef,
    delta,
    loss,
    tang,
    up_out,
    down_out,
    below_in,
    above_in,
    tiny_out,
    tiny_in,
    turn,
    adj,
    back,
    placed,
    load_sem,
    weight_sem,
    fwd_send,
    fwd_recv,
    coef_send,
    coef_recv,
    tiny_send,
    tiny_recv,
    lev_send,
    lev_recv,
    ret_recv,
):
    tracers, levels, cols = traj_hbm.shape
    rows = tracers * levels
    reach = weight_hbm.shape[1]
    win, cap = weight_hbm.shape[2], weight_hbm.shape[3]
    centre = reach // 2
    span = cols // reach
    tiles = cols // LANES
    sub = span // LANES
    me = lax.axis_index("tile")
    lev = lax.axis_index("lev")

    def tile_at(distance):
        return (lax.rem(me + (n_tile + distance), n_tile), lev)

    barrier = pltpu.get_barrier_semaphore()
    radius = centre + 1
    for distance in range(-radius, radius + 1):
        if distance != 0:
            pl.semaphore_signal(barrier, inc=1, device_id=tile_at(distance), device_id_type=MESH)

    @pl.when(lev > 0)
    def _():
        pl.semaphore_signal(barrier, inc=1, device_id=(me, lev - 1), device_id_type=MESH)

    @pl.when(lev < n_lev - 1)
    def _():
        pl.semaphore_signal(barrier, inc=1, device_id=(me, lev + 1), device_id_type=MESH)

    loads = [
        pltpu.make_async_copy(source, target, load_sem.at[i])
        for i, (source, target) in enumerate(
            (
                (counts_hbm, counts_ref),
                (kappa_hbm, kappa_ref),
                (traj_hbm, traj_ref),
                (inc_hbm, inc_ref),
                (courant_hbm, courant_ref),
                (vertical_hbm, vertical_ref),
                (offset_hbm, offset_ref),
            )
        )
    ]
    weight_copies = {
        d: pltpu.make_async_copy(weight_hbm.at[0, d], weight.at[d], sem)
        for group, sems in ((FIRST, weight_sem), (REST, load_sem))
        for d, sem in ((d, sems.at[i]) for i, d in enumerate(group))
    }
    for copy in loads:
        copy.start()
    for d in FIRST:
        weight_copies[d].start()

    for copy in loads:
        copy.wait()
    for d in REST:
        weight_copies[d].start()
    stacked = jnp.concatenate(
        [ref[m].astype(jnp.float32) for ref in (traj_ref, inc_ref) for m in range(tracers)], axis=0
    ).astype(jnp.bfloat16)
    for t in range(tiles):
        fields[t] = stacked[:, t * LANES : (t + 1) * LANES]
    for t in range(tiles, fields.shape[0]):
        fields[t] = jnp.zeros((2 * rows, LANES), jnp.bfloat16)
    vertical = vertical_ref[...]
    coef[pl.ds(0, 1), pl.ds(LANES, cols)] = courant_ref[...]
    coef[pl.ds(1, 1), pl.ds(LANES, cols)] = offset_ref[...].astype(jnp.float32)
    coef[pl.ds(2, 1), pl.ds(LANES, cols)] = jnp.maximum(vertical, 0.0)
    coef[pl.ds(3, 1), pl.ds(LANES, cols)] = jnp.maximum(-vertical, 0.0)
    coef[pl.ds(4, 4), pl.ds(LANES, cols)] = jnp.zeros((4, cols), jnp.float32)
    for ref in (up_out, down_out):
        ref[pl.ds(6, 2), :] = jnp.zeros((2, ref.shape[1]), jnp.float32)
    turn[...] = jnp.zeros_like(turn)
    for at in (0, delta.shape[1] - LANES):
        delta[:, pl.ds(at, LANES)] = jnp.zeros((rows, LANES), jnp.float32)

    @pl.when(lev == 0)
    def _():
        below_in[...] = jnp.zeros_like(below_in)

    @pl.when(lev == n_lev - 1)
    def _():
        above_in[...] = jnp.zeros_like(above_in)

    placed[:, pl.ds(0, 1)] = jnp.zeros((reach, 1, rows, LANES), jnp.float32)
    placed[:, pl.ds(placed.shape[1] - 1, 1)] = jnp.zeros((reach, 1, rows, LANES), jnp.float32)

    starts = []
    total = jnp.int32(0)
    for d in range(reach):
        starts.append(total)
        total = total + counts_ref[0, d]

    firsts = [lax.shift_right_logical(start, 7) for start in starts]
    shifts = [lax.bitwise_and(start, LANES - 1) for start in starts]
    parts = cap // LANES
    lane = lax.broadcasted_iota(jnp.int32, (2 * rows, LANES), 1)
    skew = lax.broadcasted_iota(jnp.int32, (2 * LANES, LANES), 0) - lax.broadcasted_iota(
        jnp.int32, (2 * LANES, LANES), 1
    )

    def selection(amount):
        return jnp.where(skew == amount, 1.0, 0.0).astype(jnp.bfloat16)

    def slots_of(d):
        loaded = [fields[firsts[d] + t] for t in range(parts + 1)]
        pairs = [jnp.concatenate([loaded[t], loaded[t + 1]], axis=1) for t in range(parts)]
        moved = jnp.dot(
            jnp.concatenate(pairs, axis=0), selection(shifts[d]), preferred_element_type=jnp.float32
        )
        pieces = []
        for t in range(parts):
            value = moved[t * 2 * rows : (t + 1) * 2 * rows]
            pieces.append(jnp.where(lane + t * LANES < counts_ref[0, d], value, 0.0).astype(jnp.bfloat16))
        return jnp.concatenate(pieces, axis=1)

    tall = lax.broadcasted_iota(jnp.int32, (win, LANES), 1)

    def place_weight(d):
        chosen = selection(LANES - shifts[d])
        nothing = jnp.zeros((win, LANES), jnp.bfloat16)
        live = []
        for t in range(parts):
            piece = weight[d, :, pl.ds(t * LANES, LANES)]
            live.append(jnp.where(tall + t * LANES < counts_ref[0, d], piece, nothing))
        live = [nothing, *live, nothing]
        for t in range(parts + 1):
            moved = jnp.dot(
                jnp.concatenate([live[t], live[t + 1]], axis=1), chosen, preferred_element_type=jnp.float32
            )
            shifted[d, :, pl.ds(t * LANES, LANES)] = moved.astype(jnp.bfloat16)

    parity = lax.rem(me, 2)
    half = win // 2

    def on_core(cores, run):
        if len(cores) == 2:
            run()
        else:
            pl.when(parity == cores[0])(run)

    def window_part(d, lane, width):
        part = pl.ds(lane, width)
        return outgoing.at[d, :, part], recv.at[d, :, part], d - centre

    plan = {
        "g0w": (EVEN, 0, 0, *window_part(0, 0, win)),
        "g0l": (ODD, 0, 0, *window_part(0, 0, half)),
        "g1h": (EVEN, 1, 1, *window_part(1, half, half)),
        "g1l": (ODD, 1, 1, *window_part(1, 0, half)),
        "g2h": (EVEN, 2, 2, *window_part(2, half, half)),
        "g2l": (ODD, 2, 2, *window_part(2, 0, half)),
        "g3h": (EVEN, 3, 3, *window_part(3, half, half)),
        "g3w": (ODD, 3, 3, *window_part(3, 0, win)),
        "g5w": (EVEN, 4, 4, *window_part(5, 0, win)),
        "g5l": (ODD, 4, 4, *window_part(5, 0, half)),
        "g6h": (EVEN, 5, 5, *window_part(6, half, half)),
        "g6l": (ODD, 5, 5, *window_part(6, 0, half)),
        "g7h": (EVEN, 6, 6, *window_part(7, half, half)),
        "g7w": (ODD, 6, 6, *window_part(7, 0, win)),
        "m1": (EVEN, 7, 10, outgoing.at[1, :, pl.ds(0, half)], mixing.at[0], 1),
        "m2": (EVEN, 8, 11, outgoing.at[2, :, pl.ds(0, half)], mixing.at[1], 1),
        "m3": (EVEN, 9, 12, outgoing.at[3, :, pl.ds(0, half)], mixing.at[2], 1),
        "m5": (ODD, 7, 10, outgoing.at[5, :, pl.ds(half, half)], mixing.at[0], -1),
        "m6": (ODD, 8, 11, outgoing.at[6, :, pl.ds(half, half)], mixing.at[1], -1),
        "c1": (ODD, 9, 7, summed.at[0], recv.at[1, :, pl.ds(0, half)], -4),
        "c2": (ODD, 10, 7, summed.at[1], recv.at[2, :, pl.ds(0, half)], -3),
        "c3": (ODD, 11, 8, summed.at[2], recv.at[3, :, pl.ds(0, half)], -2),
        "c6": (EVEN, 10, 8, summed.at[0], recv.at[6, :, pl.ds(0, half)], 2),
        "c7": (EVEN, 11, 9, summed.at[1], recv.at[7, :, pl.ds(0, half)], 3),
    }
    forward = {
        name: pltpu.make_async_remote_copy(
            src_ref=source,
            dst_ref=target,
            send_sem=fwd_send.at[leaving],
            recv_sem=fwd_recv.at[landing],
            device_id=tile_at(distance),
            device_id_type=MESH,
        )
        for name, (_, leaving, landing, source, target, distance) in plan.items()
    }
    corners = ((0, 0, 0, -5), (7, half, 0, 2), (7, half - 16, 8, 4), (6, win - 16, 8, 3))
    halo_parts = [
        pltpu.make_async_remote_copy(
            src_ref=tiny_out.at[i],
            dst_ref=tiny_in.at[i],
            send_sem=tiny_send.at[i],
            recv_sem=tiny_recv.at[i],
            device_id=tile_at(distance),
            device_id_type=MESH,
        )
        for i, (_, _, _, distance) in enumerate(corners)
    ]

    def send(*names):
        for name in names:
            on_core(plan[name][0], forward[name].start)

    def arrived(*names):
        for name in names:
            forward[name].wait_recv()

    giving = {
        d: pltpu.make_async_remote_copy(
            src_ref=adj.at[:, pl.ds(d * span, win)],
            dst_ref=back.at[d],
            send_sem=fwd_send.at[d if d < centre else d - 1],
            recv_sem=ret_recv.at[d],
            device_id=tile_at(centre - d),
            device_id_type=MESH,
        )
        for d in range(reach)
        if d != centre
    }

    coef_edges = [
        pltpu.make_async_remote_copy(
            src_ref=coef.at[:, pl.ds(source, LANES)],
            dst_ref=coef.at[:, pl.ds(target, LANES)],
            send_sem=coef_send.at[i],
            recv_sem=coef_recv.at[i],
            device_id=tile_at(distance),
            device_id_type=MESH,
        )
        for i, (source, target, distance) in enumerate(((LANES, LANES + cols, -1), (cols, 0, 1)))
    ]

    early = ((-1, 1), (11, tiles + 1))
    middle = ((1, 5),)
    late = ((5, 11),)
    level_up, level_down = ([], [], []), ([], [], [])
    index = 0
    for stage, ranges in enumerate((early, middle, late)):
        for lo, hi in ranges:
            part = pl.ds((lo + 1) * LANES, (hi - lo) * LANES)
            for ways, source, target, distance in (
                (level_up, up_out, below_in, 1),
                (level_down, down_out, above_in, n_lev - 1),
            ):
                ways[stage].append(
                    pltpu.make_async_remote_copy(
                        src_ref=source.at[:, part],
                        dst_ref=target.at[:, part],
                        send_sem=lev_send.at[index],
                        recv_sem=lev_recv.at[index],
                        device_id=(me, lax.rem(lev + distance, n_lev)),
                        device_id_type=MESH,
                    )
                )
                index += 1

    def level_start(stage):
        @pl.when(lev < n_lev - 1)
        def _():
            for copy in level_up[stage]:
                copy.start()

        @pl.when(lev > 0)
        def _():
            for copy in level_down[stage]:
                copy.start()

    def level_wait(stage):
        @pl.when(lev > 0)
        def _():
            for copy in level_up[stage]:
                copy.wait_recv()

        @pl.when(lev < n_lev - 1)
        def _():
            for copy in level_down[stage]:
                copy.wait_recv()

    sends = {
        0: ("g0w", "g0l"),
        7: ("g7h", "g7w"),
        6: ("m6", "g6h", "g6l"),
        1: ("m1", "g1h", "g1l"),
        2: ("m2", "g2h", "g2l"),
        3: ("m3", "g3h", "g3w"),
        5: ("m5", "g5w", "g5l"),
    }

    def windows(groups):
        slotted = {d: slots_of(d) for d in groups}
        for d in groups:
            weight_copies[d].wait()
        for i, (d, column, row, _) in enumerate(corners):
            if d in groups:
                corner = lax.dot_general(
                    weight[d, pl.ds(column, 16), :],
                    slotted[d],
                    (((1,), (1,)), ((), ())),
                    preferred_element_type=jnp.float32,
                )
                tiny_out[i, :, pl.ds(0, 2 * rows)] = corner[row : row + 8]
        for d in groups:
            window = lax.dot_general(
                slotted[d], weight[d], (((1,), (1,)), ((), ())), preferred_element_type=jnp.float32
            )
            if d == centre:
                recv[d] = window
            else:
                outgoing[d] = window

    tiny_out[...] = jnp.zeros_like(tiny_out)
    windows(FIRST)
    pl.semaphore_wait(
        barrier, 2 * radius + (lev > 0).astype(jnp.int32) + (lev < n_lev - 1).astype(jnp.int32)
    )
    for copy in (*halo_parts, *coef_edges):
        copy.start()
    for d in FIRST:
        send(*sends[d])
    windows(REST)
    for d in REST:
        if d != centre:
            send(*sends[d])
    for d in FIRST:
        place_weight(d)

    @pl.when(parity == 1)
    def _():
        for b in (1, 2, 3):
            arrived(f"m{b}")
            summed[b - 1] = outgoing[b - 1, :, pl.ds(half, half)] + mixing[b - 1]
            forward[f"c{b}"].start()

    @pl.when(parity == 0)
    def _():
        arrived("m6")
        summed[1] = outgoing[7, :, pl.ds(0, half)] + mixing[1]
        forward["c7"].start()
        arrived("m5")
        summed[0] = outgoing[6, :, pl.ds(0, half)] + mixing[0]
        forward["c6"].start()

    def finish(column, width, *pieces):
        value = None
        for d, at in pieces:
            piece = recv[d, :, pl.ds(at, width)]
            value = piece if value is None else value + piece
        for m in range(tracers):
            part = pl.ds(m * levels, levels)
            loss[part, pl.ds(LANES + column, width)] = 2.0 * kappa_ref[m] * value[m * levels : (m + 1) * levels]
        delta[:, pl.ds(2 * LANES + column, width)] = value[rows:]

    def finish_halo():
        turn[pl.ds(0, 8), :] = tiny_in[0] + tiny_in[1]
        turn[pl.ds(LANES - 8, 8), :] = tiny_in[2] + tiny_in[3]
        value = jnp.transpose(turn[...])
        for at in (0, LANES + cols):
            for m in range(tracers):
                part = pl.ds(m * levels, levels)
                loss[part, pl.ds(at, LANES)] = 2.0 * kappa_ref[m] * value[m * levels : (m + 1) * levels]
            delta[:, pl.ds(LANES + at, LANES)] = value[rows : 2 * rows]

    def level_rows(width):
        return lax.broadcasted_iota(jnp.int32, (levels, width), 0)

    def tangent_partial(lo, hi):
        width = (hi - lo) * LANES
        own = pl.ds(LANES + lo * LANES, width)
        courant, offset = coef[pl.ds(0, 1), own], coef[pl.ds(1, 1), own]
        rising, sinking = coef[pl.ds(2, 1), own], coef[pl.ds(3, 1), own]
        level = level_rows(width)
        for m in range(tracers):
            part = pl.ds(m * levels, levels)
            wide = delta[part, pl.ds((lo + 1) * LANES, width + 2 * LANES)]
            here = wide[:, LANES : LANES + width]
            departed = jnp.zeros_like(here)
            for shift in range(-HALO, HALO + 1):
                moved = here
                if shift != 0:
                    moved = pltpu.roll(wide, (-shift) % (width + 2 * LANES), 1)[:, LANES : LANES + width]
                departed = jnp.where(offset == float(shift), moved, departed)
            below = jnp.where(level == 0, 0.0, pltpu.roll(here, 1, 0))
            above = jnp.where(level == levels - 1, 0.0, pltpu.roll(here, levels - 1, 0))
            value = (
                here
                + courant * (departed - here)
                + rising * (below - here)
                + sinking * (above - here)
                - loss[part, own] * here
            )
            tang[part, own] = value
            up_out[pl.ds(m, 1), own] = value[levels - 1 : levels]
            up_out[pl.ds(tracers + m, 1), own] = here[levels - 1 : levels]
            down_out[pl.ds(m, 1), own] = value[0:1]
            down_out[pl.ds(tracers + m, 1), own] = here[0:1]

    def tangent_finish(lo, hi):
        width = (hi - lo) * LANES
        own = pl.ds(LANES + lo * LANES, width)
        rising, sinking = coef[pl.ds(2, 1), own], coef[pl.ds(3, 1), own]
        level = level_rows(width)
        inner_lo, inner_hi = max(lo, 0), min(hi, tiles)
        for m in range(tracers):
            part = pl.ds(m * levels, levels)
            value = tang[part, own]
            value = value + jnp.where(level == 0, rising * below_in[pl.ds(tracers + m, 1), own], 0.0)
            value = value + jnp.where(level == levels - 1, sinking * above_in[pl.ds(tracers + m, 1), own], 0.0)
            tang[part, own] = value
            tangent_out[m, :, pl.ds(inner_lo * LANES, (inner_hi - inner_lo) * LANES)] = value[
                :, (inner_lo - lo) * LANES : (inner_hi - lo) * LANES
            ]

    def adjoint(lo, hi):
        width = (hi - lo) * LANES
        own = pl.ds(LANES + lo * LANES, width)
        out = pl.ds(lo * LANES, width)
        around = pl.ds(lo * LANES, width + 2 * LANES)
        courant, rising, sinking = coef[pl.ds(0, 1), own], coef[pl.ds(2, 1), own], coef[pl.ds(3, 1), own]
        wide_courant, wide_offset = coef[pl.ds(0, 1), around], coef[pl.ds(1, 1), around]
        level = level_rows(width)
        pieces = []
        for m in range(tracers):
            part = pl.ds(m * levels, levels)
            wide = tang[part, around]
            here = wide[:, LANES : LANES + width]
            total = jnp.zeros_like(here)
            for shift in range(-HALO, HALO + 1):
                term = jnp.where(wide_offset == float(shift), wide_courant, 0.0) * wide
                if shift != 0:
                    term = pltpu.roll(term, shift % (width + 2 * LANES), 1)
                total = total + term[:, LANES : LANES + width]
            own_delta = delta[part, pl.ds((lo + 2) * LANES, width)]
            under = below_in[pl.ds(m, 1), own] + sinking * own_delta[0:1]
            over = above_in[pl.ds(m, 1), own] + rising * own_delta[levels - 1 : levels]
            under = jnp.where(lev > 0, under, 0.0)
            over = jnp.where(lev < n_lev - 1, over, 0.0)
            lower = jnp.where(level == 0, under, pltpu.roll(here, 1, 0))
            upper = jnp.where(level == levels - 1, over, pltpu.roll(here, levels - 1, 0))
            diagonal = 1.0 - courant - rising - sinking - loss[part, own]
            pieces.append(diagonal * here + total + rising * upper + sinking * lower)
        value = jnp.concatenate(pieces, axis=0).astype(jnp.bfloat16)
        adj[:, out] = value
        if lo == 0:
            adj[:, pl.ds(cols, span)] = value[:, :span]

    for d in REST:
        place_weight(d)
    for copy in (*halo_parts, *coef_edges):
        copy.wait_recv()
    finish_halo()

    @pl.when(parity == 0)
    def _():
        arrived("g0w", "g7w", "g6h", "g5l", "c6")
        finish(0, span, (0, 0), (7, half))
        finish(7 * span, span, (7, 0), (6, half))
        finish(5 * span, span, (5, 0), (4, half))
        finish(6 * span, span, (6, 0))

    @pl.when(parity == 1)
    def _():
        arrived("g0l", "g7h", "c7", "g6l", "g5w")
        finish(0, span, (0, 0), (7, half))
        finish(7 * span, span, (7, 0))
        finish(5 * span, span, (5, 0), (4, half))
        finish(6 * span, span, (6, 0), (5, half))

    for lo, hi in early:
        tangent_partial(lo, hi)
    level_start(0)

    @pl.when(parity == 0)
    def _():
        arrived("g1l", "c2")
        finish(span, span, (1, 0), (0, half))
        finish(2 * span, span, (2, 0))

    @pl.when(parity == 1)
    def _():
        arrived("c1", "g2l", "g1h")
        finish(span, span, (1, 0))
        finish(2 * span, span, (2, 0), (1, half))

    for lo, hi in middle:
        tangent_partial(lo, hi)
    level_start(1)

    @pl.when(parity == 0)
    def _():
        arrived("g2h", "g3w")
        finish(3 * span, span, (3, 0), (2, half))
        finish(4 * span, span, (4, 0), (3, half))

    @pl.when(parity == 1)
    def _():
        arrived("g3h", "c3")
        finish(3 * span, span, (3, 0))
        finish(4 * span, span, (4, 0), (3, half))

    for lo, hi in late:
        tangent_partial(lo, hi)
    level_start(2)
    level_wait(0)
    for lo, hi in early:
        tangent_finish(lo, hi)
    level_wait(1)
    for lo, hi in middle:
        tangent_finish(lo, hi)
    adjoint(0, 4)
    adjoint(12, tiles)
    for name, copy in forward.items():
        on_core(plan[name][0], copy.wait_send)
    for d in (0, 7, 6):
        giving[d].start()
    level_wait(2)
    for lo, hi in late:
        tangent_finish(lo, hi)
    adjoint(4, 12)
    for d in (1, 2, 5, 3):
        giving[d].start()

    def grads(groups):
        for d in groups:
            if d != centre:
                giving[d].wait_recv()
        for d in groups:
            returned = adj[:, pl.ds(d * span, win)] if d == centre else back[d]
            grad = jnp.dot(returned, shifted[d], preferred_element_type=jnp.float32)
            for t in range(parts + 1):
                placed[d, t + 1] = grad[:, t * LANES : (t + 1) * LANES]

    grads((centre, 0, 7, 6))
    grads((1, 2, 5, 3))

    top = placed.shape[1] - 1
    for t in range(tiles):
        value = None
        for d in range(reach):
            at = lax.min(lax.max(t + 1 - firsts[d], 0), top)
            piece = placed[d, at]
            value = piece if value is None else value + piece
        for m in range(tracers):
            grad_out[m, :, pl.ds(t * LANES, LANES)] = value[m * levels : (m + 1) * levels]

    for copy in (*giving.values(), *coef_edges, *halo_parts):
        copy.wait_send()

    @pl.when(lev < n_lev - 1)
    def _():
        for copies in level_up:
            for copy in copies:
                copy.wait_send()

    @pl.when(lev > 0)
    def _():
        for copies in level_down:
            for copy in copies:
                copy.wait_send()


def shards(n_tile, n_lev, trajectory, increment, counts, remap_weight, kappa, courant, vertical, offset):
    tracers, levels, cols = trajectory.shape
    reach, win, cap = remap_weight.shape[1:]
    rows = tracers * levels
    span = cols // reach
    wide = cols + 2 * LANES
    f32, bf16 = jnp.float32, jnp.bfloat16
    vmem = pl.BlockSpec(memory_space=pltpu.VMEM)
    dma = pltpu.SemaphoreType.DMA
    out = jax.ShapeDtypeStruct((tracers, levels, cols), f32)
    return pl.pallas_call(
        functools.partial(kernel, n_tile, n_lev),
        out_shape=(out, out),
        in_specs=[pl.BlockSpec(memory_space=pltpu.HBM)] * 8,
        out_specs=(vmem, vmem),
        scratch_shapes=[
            pltpu.VMEM((tracers, levels, cols), bf16),
            pltpu.VMEM((tracers, levels, cols), bf16),
            pltpu.SMEM((1, reach), jnp.int32),
            pltpu.SMEM((tracers,), f32),
            pltpu.VMEM((1, cols), f32),
            pltpu.VMEM((1, cols), f32),
            pltpu.VMEM((1, cols), jnp.int32),
            pltpu.VMEM((reach, win, cap), bf16),
            pltpu.VMEM((reach, win, cap + LANES), bf16),
            pltpu.VMEM((cols // LANES + cap // LANES + 1, 2 * rows, LANES), bf16),
            pltpu.VMEM((reach, 2 * rows, win), f32),
            pltpu.VMEM((3, 2 * rows, win // 2), f32),
            pltpu.VMEM((3, 2 * rows, win // 2), f32),
            pltpu.VMEM((reach, 2 * rows, win), f32),
            pltpu.VMEM((8, wide), f32),
            pltpu.VMEM((rows, wide + 2 * LANES), f32),
            pltpu.VMEM((rows, wide), f32),
            pltpu.VMEM((rows, wide), f32),
            pltpu.VMEM((8, wide), f32),
            pltpu.VMEM((8, wide), f32),
            pltpu.VMEM((8, wide), f32),
            pltpu.VMEM((8, wide), f32),
            pltpu.VMEM((4, 8, LANES), f32),
            pltpu.VMEM((4, 8, LANES), f32),
            pltpu.VMEM((LANES, LANES), f32),
            pltpu.VMEM((rows, cols + span), bf16),
            pltpu.VMEM((reach, rows, win), bf16),
            pltpu.VMEM((reach, cap // LANES + 3, rows, LANES), f32),
            dma((7,)),
            dma((len(FIRST),)),
            dma((12,)),
            dma((13,)),
            dma((2,)),
            dma((2,)),
            dma((4,)),
            dma((4,)),
            dma((8,)),
            dma((8,)),
            dma((reach,)),
        ],
        compiler_params=pltpu.CompilerParams(
            collective_id=0, has_side_effects=True, vmem_limit_bytes=24 * 1024 * 1024
        ),
    )(
        *(
            pltpu.with_memory_space_constraint(operand, pltpu.HBM)
            for operand in (
                trajectory,
                increment,
                counts,
                kappa,
                courant.reshape(1, cols),
                vertical.reshape(1, cols),
                offset.reshape(1, cols),
                remap_weight,
            )
        )
    )


def solution(mesh):
    return jax.shard_map(
        functools.partial(shards, mesh.shape["tile"], mesh.shape["lev"]),
        mesh=mesh,
        in_specs=(
            P(None, "lev", "tile"),
            P(None, "lev", "tile"),
            P("tile", None),
            P("tile", None, None, None),
            P(),
            P("tile"),
            P("tile"),
            P("tile"),
        ),
        out_specs=(P(None, "lev", "tile"), P(None, "lev", "tile")),
        check_vma=False,
    )
```

time: 40.8 us -> 37.9 us (0.929)
  Pallas kernels: 38.6 us -> 35.7 us
    pallas_call x1, Pallas kernels: 38.6 us -> 35.7 us  [shards(): pl.pallas_call(functools.partial(kernel, n_tile, n_lev), out_shape=(out,...]
where the time goes in v4:
time: 37.9 us; the launch traced here: 37.7 us
  Pallas kernels  35.7 us (94%)
  local copies, waits for them, and re-layouts  1.36 us (4%)
  between operations  0.64 us (2%)
    pallas_call x1, Pallas kernels, shards(): pl.pallas_call(functools.partial(kernel, n_tile, n_lev), out_shape=(out,...  35.7 us
    unnamed x2, local copies, waits for them, and re-layouts  1.36 us

profile of v4, /device:TPU:1, one launch (start us, length us, event | category | flops | bytes accessed | tf_op | source)
XLA Modules:
  0.0 37.7 jit_solution(5519100837446414351)
XLA Ops:
  0.6 35.7 %shard_map.95 = (f32[3,8,2048]{2,1,0:T(8,128)S(1)}, f32[3,8,2048]{2,1,0:T(8,128)S(1)}) custom-call(bf16[3,8,2048]{2,1,0:T(8,128)(2,1)} %traj_hbm.1, bf16[3,8,2048]{2,1,0:T(8,128)(2,1)} %inc_hbm.1, s32[1,8]{1,0:T(1,128)} %counts_hbm.1, f32[3]{0:T(128)} %kappa_hbm.1, f32[1,2048]{1,0:T(1,128)} %bitcast.3, f32[1,2048]{1,0:T(1,128)} %bitcast.4, ...), custom_call_target="tpu_custom_call" | custom-call | tf_op jit(solution)/shard_map/pallas_call | solution.py:636
  36.4 0.7 %copy.12 = f32[3,8,2048]{2,1,0:T(8,128)} copy(f32[3,8,2048]{2,1,0:T(8,128)S(1)} %get-tuple-element.4) | data formatting | bytes 393216
  37.0 0.7 %copy.13 = f32[3,8,2048]{2,1,0:T(8,128)} copy(f32[3,8,2048]{2,1,0:T(8,128)S(1)} %get-tuple-element.5) | data formatting | bytes 393216

commit v5 on v4

--- a/solution.py
+++ b/solution.py
@@ -10,7 +10,8 @@
 MESH = pl.DeviceIdType.MESH
 LANES = 128
 HALO = 2
-FIRST, REST = (0, 7, 6), (1, 2, 3, 5, 4)
+FIRST, SECOND, THIRD = (0,), (1, 2, 3), (7, 6, 5, 4)
+REST = SECOND + THIRD
 EVEN, ODD = (0,), (1,)
 BOTH = (0, 1)
 
@@ -213,12 +214,8 @@
         return outgoing.at[d, :, part], recv.at[d, :, part], d - centre
 
     plan = {
-        "g0w": (EVEN, 0, 0, *window_part(0, 0, win)),
-        "g0l": (ODD, 0, 0, *window_part(0, 0, half)),
-        "g1h": (EVEN, 1, 1, *window_part(1, half, half)),
-        "g1l": (ODD, 1, 1, *window_part(1, 0, half)),
+        "g0l": (BOTH, 0, 0, *window_part(0, 0, half)),
         "g2h": (EVEN, 2, 2, *window_part(2, half, half)),
-        "g2l": (ODD, 2, 2, *window_part(2, 0, half)),
         "g3h": (EVEN, 3, 3, *window_part(3, half, half)),
         "g3w": (ODD, 3, 3, *window_part(3, 0, win)),
         "g5w": (EVEN, 4, 4, *window_part(5, 0, win)),
@@ -232,6 +229,10 @@
         "m3": (EVEN, 9, 12, outgoing.at[3, :, pl.ds(0, half)], mixing.at[2], 1),
         "m5": (ODD, 7, 10, outgoing.at[5, :, pl.ds(half, half)], mixing.at[0], -1),
         "m6": (ODD, 8, 11, outgoing.at[6, :, pl.ds(half, half)], mixing.at[1], -1),
+        "t0": (EVEN, 1, 1, outgoing.at[0, :, pl.ds(half, half)], mixing.at[3], -1),
+        "t1": (EVEN, 12, 13, outgoing.at[1, :, pl.ds(half, half)], mixing.at[4], -1),
+        "u1": (ODD, 1, 1, summed.at[3], recv.at[1, :, pl.ds(0, half)], -3),
+        "u2": (ODD, 2, 2, summed.at[4], recv.at[2, :, pl.ds(0, half)], -2),
         "c1": (ODD, 9, 7, summed.at[0], recv.at[1, :, pl.ds(0, half)], -4),
         "c2": (ODD, 10, 7, summed.at[1], recv.at[2, :, pl.ds(0, half)], -3),
         "c3": (ODD, 11, 8, summed.at[2], recv.at[3, :, pl.ds(0, half)], -2),
@@ -342,11 +343,11 @@
                 copy.wait_recv()
 
     sends = {
-        0: ("g0w", "g0l"),
+        0: ("g0l", "t0"),
         7: ("g7h", "g7w"),
         6: ("m6", "g6h", "g6l"),
-        1: ("m1", "g1h", "g1l"),
-        2: ("m2", "g2h", "g2l"),
+        1: ("m1", "t1"),
+        2: ("m2", "g2h"),
         3: ("m3", "g3h", "g3w"),
         5: ("m5", "g5w", "g5l"),
     }
@@ -378,23 +379,36 @@
     pl.semaphore_wait(
         barrier, 2 * radius + (lev > 0).astype(jnp.int32) + (lev < n_lev - 1).astype(jnp.int32)
     )
-    for copy in (*halo_parts, *coef_edges):
+    for copy in coef_edges:
         copy.start()
-    for d in FIRST:
-        send(*sends[d])
-    windows(REST)
-    for d in REST:
-        if d != centre:
-            send(*sends[d])
-    for d in FIRST:
+
+    def send_group(group):
+        for copy, corner in zip(halo_parts, corners):
+            if corner[0] in group:
+                copy.start()
+        for d in group:
+            if d != centre:
+                send(*sends[d])
+
+    send_group(FIRST)
+    for group in (SECOND, THIRD):
+        windows(group)
+        send_group(group)
+    for d in SECOND:
         place_weight(d)
 
     @pl.when(parity == 1)
     def _():
-        for b in (1, 2, 3):
-            arrived(f"m{b}")
-            summed[b - 1] = outgoing[b - 1, :, pl.ds(half, half)] + mixing[b - 1]
-            forward[f"c{b}"].start()
+        for name, slot, d, at, sum_name in (
+            ("m1", 0, 0, half, "c1"),
+            ("t0", 3, 1, 0, "u1"),
+            ("m2", 1, 1, half, "c2"),
+            ("t1", 4, 2, 0, "u2"),
+            ("m3", 2, 2, half, "c3"),
+        ):
+            forward[name].wait_recv()
+            summed[slot] = outgoing[d, :, pl.ds(at, half)] + mixing[slot]
+            forward[sum_name].start()
 
     @pl.when(parity == 0)
     def _():
@@ -508,7 +522,7 @@
         if lo == 0:
             adj[:, pl.ds(cols, span)] = value[:, :span]
 
-    for d in REST:
+    for d in FIRST + THIRD:
         place_weight(d)
     for copy in (*halo_parts, *coef_edges):
         copy.wait_recv()
@@ -516,7 +530,7 @@
 
     @pl.when(parity == 0)
     def _():
-        arrived("g0w", "g7w", "g6h", "g5l", "c6")
+        arrived("g0l", "g7w", "g6h", "g5l", "c6")
         finish(0, span, (0, 0), (7, half))
         finish(7 * span, span, (7, 0), (6, half))
         finish(5 * span, span, (5, 0), (4, half))
@@ -536,15 +550,15 @@
 
     @pl.when(parity == 0)
     def _():
-        arrived("g1l", "c2")
-        finish(span, span, (1, 0), (0, half))
+        arrived("u1", "c2")
+        finish(span, span, (1, 0))
         finish(2 * span, span, (2, 0))
 
     @pl.when(parity == 1)
     def _():
-        arrived("c1", "g2l", "g1h")
+        arrived("c1", "u2")
         finish(span, span, (1, 0))
-        finish(2 * span, span, (2, 0), (1, half))
+        finish(2 * span, span, (2, 0))
 
     for lo, hi in middle:
         tangent_partial(lo, hi)
@@ -594,18 +608,23 @@
             for t in range(parts + 1):
                 placed[d, t + 1] = grad[:, t * LANES : (t + 1) * LANES]
 
-    grads((centre, 0, 7, 6))
-    grads((1, 2, 5, 3))
-
     top = placed.shape[1] - 1
-    for t in range(tiles):
-        value = None
-        for d in range(reach):
-            at = lax.min(lax.max(t + 1 - firsts[d], 0), top)
-            piece = placed[d, at]
-            value = piece if value is None else value + piece
-        for m in range(tracers):
-            grad_out[m, :, pl.ds(t * LANES, LANES)] = value[m * levels : (m + 1) * levels]
+
+    def unslot(groups, again):
+        for t in range(tiles):
+            value = None
+            for d in groups:
+                piece = placed[d, lax.min(lax.max(t + 1 - firsts[d], 0), top)]
+                value = piece if value is None else value + piece
+            for m in range(tracers):
+                part = value[m * levels : (m + 1) * levels]
+                if again:
+                    part = part + grad_out[m, :, pl.ds(t * LANES, LANES)]
+                grad_out[m, :, pl.ds(t * LANES, LANES)] = part
+
+    for again, groups in ((False, (centre, 0, 7, 6)), (True, (1, 2, 5, 3))):
+        grads(groups)
+        unslot(groups, again)
 
     for copy in (*giving.values(), *coef_edges, *halo_parts):
         copy.wait_send()
@@ -621,6 +640,17 @@
         for copies in level_down:
             for copy in copies:
                 copy.wait_send()
+
+
+def store(tangent_ref, grad_ref, tangent_hbm, grad_hbm, sem):
+    copies = [
+        pltpu.make_async_copy(tangent_ref, tangent_hbm, sem.at[0]),
+        pltpu.make_async_copy(grad_ref, grad_hbm, sem.at[1]),
+    ]
+    for copy in copies:
+        copy.start()
+    for copy in copies:
+        copy.wait()
 
 
 def shards(n_tile, n_lev, trajectory, increment, counts, remap_weight, kappa, courant, vertical, offset):
@@ -633,7 +663,7 @@
     vmem = pl.BlockSpec(memory_space=pltpu.VMEM)
     dma = pltpu.SemaphoreType.DMA
     out = jax.ShapeDtypeStruct((tracers, levels, cols), f32)
-    return pl.pallas_call(
+    results = pl.pallas_call(
         functools.partial(kernel, n_tile, n_lev),
         out_shape=(out, out),
         in_specs=[pl.BlockSpec(memory_space=pltpu.HBM)] * 8,
@@ -650,8 +680,8 @@
             pltpu.VMEM((reach, win, cap + LANES), bf16),
             pltpu.VMEM((cols // LANES + cap // LANES + 1, 2 * rows, LANES), bf16),
             pltpu.VMEM((reach, 2 * rows, win), f32),
-            pltpu.VMEM((3, 2 * rows, win // 2), f32),
-            pltpu.VMEM((3, 2 * rows, win // 2), f32),
+            pltpu.VMEM((5, 2 * rows, win // 2), f32),
+            pltpu.VMEM((5, 2 * rows, win // 2), f32),
             pltpu.VMEM((reach, 2 * rows, win), f32),
             pltpu.VMEM((8, wide), f32),
             pltpu.VMEM((rows, wide + 2 * LANES), f32),
@@ -669,8 +699,8 @@
             pltpu.VMEM((reach, cap // LANES + 3, rows, LANES), f32),
             dma((7,)),
             dma((len(FIRST),)),
-            dma((12,)),
             dma((13,)),
+            dma((14,)),
             dma((2,)),
             dma((2,)),
             dma((4,)),
@@ -697,6 +727,14 @@
             )
         )
     )
+    return pl.pallas_call(
+        store,
+        out_shape=(out, out),
+        in_specs=(vmem, vmem),
+        out_specs=[pl.BlockSpec(memory_space=pltpu.HBM)] * 2,
+        scratch_shapes=[dma((2,))],
+        compiler_params=pltpu.CompilerParams(vmem_limit_bytes=1024 * 1024),
+    )(*results)
 
 
 def solution(mesh):

time: 37.9 us -> 36.4 us (0.960)
  local copies, waits for them, and re-layouts: 1.36 us -> 0 us
    unnamed x2 -> x0, local copies, waits for them, and re-layouts: 1.36 us -> none
    pallas_call x1, Pallas kernels: 35.7 us -> 34.8 us  [shards(): pl.pallas_call(functools.partial(kernel, n_tile, n_lev), out_shape=(out,...]
    pallas_call x0 -> x1, Pallas kernels: none -> 0.76 us  [shards(): pl.pallas_call(store, out_shape=(out, out), in_specs=(vmem, vmem), out_sp...]
where the time goes in v5:
time: 36.4 us; the launch traced here: 36.2 us
  Pallas kernels  35.6 us (98%)
  between operations  0.64 us (2%)
    pallas_call x1, Pallas kernels, shards(): pl.pallas_call(functools.partial(kernel, n_tile, n_lev), out_shape=(out,...  34.8 us
    pallas_call x1, Pallas kernels, shards(): pl.pallas_call(store, out_shape=(out, out), in_specs=(vmem, vmem), out_sp...  0.76 us

profile of v5, /device:TPU:1, one launch (start us, length us, event | category | flops | bytes accessed | tf_op | source)
XLA Modules:
  0.0 36.2 jit_solution(1309185382020644371)
XLA Ops:
  0.6 34.8 %shard_map.95 = (f32[3,8,2048]{2,1,0:T(8,128)S(1)}, f32[3,8,2048]{2,1,0:T(8,128)S(1)}) custom-call(bf16[3,8,2048]{2,1,0:T(8,128)(2,1)} %traj_hbm.1, bf16[3,8,2048]{2,1,0:T(8,128)(2,1)} %inc_hbm.1, s32[1,8]{1,0:T(1,128)} %counts_hbm.1, f32[3]{0:T(128)} %kappa_hbm.1, f32[1,2048]{1,0:T(1,128)} %bitcast.3, f32[1,2048]{1,0:T(1,128)} %bitcast.4, ...), custom_call_target="tpu_custom_call" | custom-call | tf_op jit(solution)/shard_map/pallas_call | solution.py:666
  35.5 0.8 %shard_map.96 = (f32[3,8,2048]{2,1,0:T(8,128)}, f32[3,8,2048]{2,1,0:T(8,128)}) custom-call(f32[3,8,2048]{2,1,0:T(8,128)S(1)} %get-tuple-element.4.tangent_ref, f32[3,8,2048]{2,1,0:T(8,128)S(1)} %get-tuple-element.5.grad_ref), custom_call_target="tpu_custom_call" | custom-call | tf_op jit(solution)/shard_map/pallas_call | solution.py:730

commit v6 on v5

--- a/solution.py
+++ b/solution.py
@@ -10,7 +10,7 @@
 MESH = pl.DeviceIdType.MESH
 LANES = 128
 HALO = 2
-FIRST, SECOND, THIRD = (0,), (1, 2, 3), (7, 6, 5, 4)
+FIRST, SECOND, THIRD = (0,), (7, 6, 1), (2, 3, 5, 4)
 REST = SECOND + THIRD
 EVEN, ODD = (0,), (1,)
 BOTH = (0, 1)
@@ -220,15 +220,14 @@
         "g3w": (ODD, 3, 3, *window_part(3, 0, win)),
         "g5w": (EVEN, 4, 4, *window_part(5, 0, win)),
         "g5l": (ODD, 4, 4, *window_part(5, 0, half)),
-        "g6h": (EVEN, 5, 5, *window_part(6, half, half)),
         "g6l": (ODD, 5, 5, *window_part(6, 0, half)),
-        "g7h": (EVEN, 6, 6, *window_part(7, half, half)),
-        "g7w": (ODD, 6, 6, *window_part(7, 0, win)),
+        "g7h": (BOTH, 6, 6, *window_part(7, half, half)),
         "m1": (EVEN, 7, 10, outgoing.at[1, :, pl.ds(0, half)], mixing.at[0], 1),
         "m2": (EVEN, 8, 11, outgoing.at[2, :, pl.ds(0, half)], mixing.at[1], 1),
         "m3": (EVEN, 9, 12, outgoing.at[3, :, pl.ds(0, half)], mixing.at[2], 1),
         "m5": (ODD, 7, 10, outgoing.at[5, :, pl.ds(half, half)], mixing.at[0], -1),
         "m6": (ODD, 8, 11, outgoing.at[6, :, pl.ds(half, half)], mixing.at[1], -1),
+        "v7": (ODD, 12, 12, outgoing.at[7, :, pl.ds(0, half)], mixing.at[5], 1),
         "t0": (EVEN, 1, 1, outgoing.at[0, :, pl.ds(half, half)], mixing.at[3], -1),
         "t1": (EVEN, 12, 13, outgoing.at[1, :, pl.ds(half, half)], mixing.at[4], -1),
         "u1": (ODD, 1, 1, summed.at[3], recv.at[1, :, pl.ds(0, half)], -3),
@@ -236,6 +235,7 @@
         "c1": (ODD, 9, 7, summed.at[0], recv.at[1, :, pl.ds(0, half)], -4),
         "c2": (ODD, 10, 7, summed.at[1], recv.at[2, :, pl.ds(0, half)], -3),
         "c3": (ODD, 11, 8, summed.at[2], recv.at[3, :, pl.ds(0, half)], -2),
+        "w7": (EVEN, 5, 5, summed.at[2], recv.at[7, :, pl.ds(0, half)], 2),
         "c6": (EVEN, 10, 8, summed.at[0], recv.at[6, :, pl.ds(0, half)], 2),
         "c7": (EVEN, 11, 9, summed.at[1], recv.at[7, :, pl.ds(0, half)], 3),
     }
@@ -343,9 +343,9 @@
                 copy.wait_recv()
 
     sends = {
-        0: ("g0l", "t0"),
-        7: ("g7h", "g7w"),
-        6: ("m6", "g6h", "g6l"),
+        0: ("t0", "g0l"),
+        7: ("v7", "g7h"),
+        6: ("m6", "g6l"),
         1: ("m1", "t1"),
         2: ("m2", "g2h"),
         3: ("m3", "g3h", "g3w"),
@@ -394,30 +394,41 @@
     for group in (SECOND, THIRD):
         windows(group)
         send_group(group)
-    for d in SECOND:
+    def add(name, slot, d, at, sum_name, mixed):
+        forward[name].wait_recv()
+        summed[slot] = outgoing[d, :, pl.ds(at, half)] + mixing[mixed]
+        forward[sum_name].start()
+
+    for d in (7, 6, 1):
         place_weight(d)
 
     @pl.when(parity == 1)
     def _():
-        for name, slot, d, at, sum_name in (
-            ("m1", 0, 0, half, "c1"),
-            ("t0", 3, 1, 0, "u1"),
-            ("m2", 1, 1, half, "c2"),
-            ("t1", 4, 2, 0, "u2"),
-            ("m3", 2, 2, half, "c3"),
-        ):
-            forward[name].wait_recv()
-            summed[slot] = outgoing[d, :, pl.ds(at, half)] + mixing[slot]
-            forward[sum_name].start()
+        add("m1", 0, 0, half, "c1", 0)
+        add("m2", 1, 1, half, "c2", 1)
+        add("m3", 2, 2, half, "c3", 2)
 
     @pl.when(parity == 0)
     def _():
-        arrived("m6")
-        summed[1] = outgoing[7, :, pl.ds(0, half)] + mixing[1]
-        forward["c7"].start()
-        arrived("m5")
-        summed[0] = outgoing[6, :, pl.ds(0, half)] + mixing[0]
-        forward["c6"].start()
+        add("m6", 1, 7, 0, "c7", 1)
+        add("v7", 2, 6, half, "w7", 5)
+        add("m5", 0, 6, 0, "c6", 0)
+
+    for d in (0, 2):
+        place_weight(d)
+
+    @pl.when(parity == 1)
+    def _():
+        add("t0", 3, 1, 0, "u1", 3)
+
+    for d in (3, 5):
+        place_weight(d)
+
+    @pl.when(parity == 1)
+    def _():
+        add("t1", 4, 2, 0, "u2", 4)
+
+    place_weight(centre)
 
     def finish(column, width, *pieces):
         value = None
@@ -522,17 +533,15 @@
         if lo == 0:
             adj[:, pl.ds(cols, span)] = value[:, :span]
 
-    for d in FIRST + THIRD:
-        place_weight(d)
     for copy in (*halo_parts, *coef_edges):
         copy.wait_recv()
     finish_halo()
 
     @pl.when(parity == 0)
     def _():
-        arrived("g0l", "g7w", "g6h", "g5l", "c6")
+        arrived("g0l", "g7h", "w7", "g5l", "c6")
         finish(0, span, (0, 0), (7, half))
-        finish(7 * span, span, (7, 0), (6, half))
+        finish(7 * span, span, (7, 0))
         finish(5 * span, span, (5, 0), (4, half))
         finish(6 * span, span, (6, 0))
 
@@ -582,20 +591,29 @@
     level_wait(0)
     for lo, hi in early:
         tangent_finish(lo, hi)
+    for core in BOTH:
+
+        @pl.when(parity == core)
+        def _():
+            for name, copy in forward.items():
+                if core in plan[name][0]:
+                    copy.wait_send()
+
     level_wait(1)
     for lo, hi in middle:
         tangent_finish(lo, hi)
     adjoint(0, 4)
+    giving[0].start()
     adjoint(12, tiles)
-    for name, copy in forward.items():
-        on_core(plan[name][0], copy.wait_send)
-    for d in (0, 7, 6):
+    for d in (7, 6):
         giving[d].start()
     level_wait(2)
     for lo, hi in late:
         tangent_finish(lo, hi)
-    adjoint(4, 12)
-    for d in (1, 2, 5, 3):
+    adjoint(4, 6)
+    giving[1].start()
+    adjoint(6, 12)
+    for d in (2, 5, 3):
         giving[d].start()
 
     def grads(groups):
@@ -622,7 +640,7 @@
                     part = part + grad_out[m, :, pl.ds(t * LANES, LANES)]
                 grad_out[m, :, pl.ds(t * LANES, LANES)] = part
 
-    for again, groups in ((False, (centre, 0, 7, 6)), (True, (1, 2, 5, 3))):
+    for again, groups in ((False, (centre, 3, 5, 6)), (True, (2, 7)), (True, (1, 0))):
         grads(groups)
         unslot(groups, again)
 
@@ -680,7 +698,7 @@
             pltpu.VMEM((reach, win, cap + LANES), bf16),
             pltpu.VMEM((cols // LANES + cap // LANES + 1, 2 * rows, LANES), bf16),
             pltpu.VMEM((reach, 2 * rows, win), f32),
-            pltpu.VMEM((5, 2 * rows, win // 2), f32),
+            pltpu.VMEM((6, 2 * rows, win // 2), f32),
             pltpu.VMEM((5, 2 * rows, win // 2), f32),
             pltpu.VMEM((reach, 2 * rows, win), f32),
             pltpu.VMEM((8, wide), f32),

time: 36.4 us -> 35.8 us (0.984)
  Pallas kernels: 35.6 us -> 35 us
    pallas_call x1, Pallas kernels: 34.8 us -> 34.3 us  [shards(): pl.pallas_call(functools.partial(kernel, n_tile, n_lev), out_shape=(out,...]
where the time goes in v6:
time: 35.8 us; the launch traced here: 35.7 us
  Pallas kernels  35 us (98%)
  between operations  0.64 us (2%)
    pallas_call x1, Pallas kernels, shards(): pl.pallas_call(functools.partial(kernel, n_tile, n_lev), out_shape=(out,...  34.3 us
    pallas_call x1, Pallas kernels, shards(): pl.pallas_call(store, out_shape=(out, out), in_specs=(vmem, vmem), out_sp...  0.76 us

profile of v6, /device:TPU:1, one launch (start us, length us, event | category | flops | bytes accessed | tf_op | source)
XLA Modules:
  0.0 35.7 jit_solution(7570722775699518493)
XLA Ops:
  0.6 34.3 %shard_map.95 = (f32[3,8,2048]{2,1,0:T(8,128)S(1)}, f32[3,8,2048]{2,1,0:T(8,128)S(1)}) custom-call(bf16[3,8,2048]{2,1,0:T(8,128)(2,1)} %traj_hbm.1, bf16[3,8,2048]{2,1,0:T(8,128)(2,1)} %inc_hbm.1, s32[1,8]{1,0:T(1,128)} %counts_hbm.1, f32[3]{0:T(128)} %kappa_hbm.1, f32[1,2048]{1,0:T(1,128)} %bitcast.3, f32[1,2048]{1,0:T(1,128)} %bitcast.4, ...), custom_call_target="tpu_custom_call" | custom-call | tf_op jit(solution)/shard_map/pallas_call | solution.py:684
  34.9 0.8 %shard_map.96 = (f32[3,8,2048]{2,1,0:T(8,128)}, f32[3,8,2048]{2,1,0:T(8,128)}) custom-call(f32[3,8,2048]{2,1,0:T(8,128)S(1)} %get-tuple-element.4.tangent_ref, f32[3,8,2048]{2,1,0:T(8,128)S(1)} %get-tuple-element.5.grad_ref), custom_call_target="tpu_custom_call" | custom-call | tf_op jit(solution)/shard_map/pallas_call | solution.py:748

commit v7 on v6

--- a/solution.py
+++ b/solution.py
@@ -243,20 +243,20 @@
         name: pltpu.make_async_remote_copy(
             src_ref=source,
             dst_ref=target,
-            send_sem=fwd_send.at[leaving],
+            send_sem=fwd_send,
             recv_sem=fwd_recv.at[landing],
             device_id=tile_at(distance),
             device_id_type=MESH,
         )
-        for name, (_, leaving, landing, source, target, distance) in plan.items()
+        for name, (_, _, landing, source, target, distance) in plan.items()
     }
     corners = ((0, 0, 0, -5), (7, half, 0, 2), (7, half - 16, 8, 4), (6, win - 16, 8, 3))
     halo_parts = [
         pltpu.make_async_remote_copy(
             src_ref=tiny_out.at[i],
             dst_ref=tiny_in.at[i],
-            send_sem=tiny_send.at[i],
-            recv_sem=tiny_recv.at[i],
+            send_sem=tiny_send,
+            recv_sem=tiny_recv,
             device_id=tile_at(distance),
             device_id_type=MESH,
         )
@@ -275,7 +275,7 @@
         d: pltpu.make_async_remote_copy(
             src_ref=adj.at[:, pl.ds(d * span, win)],
             dst_ref=back.at[d],
-            send_sem=fwd_send.at[d if d < centre else d - 1],
+            send_sem=fwd_send,
             recv_sem=ret_recv.at[d],
             device_id=tile_at(centre - d),
             device_id_type=MESH,
@@ -304,21 +304,38 @@
     for stage, ranges in enumerate((early, middle, late)):
         for lo, hi in ranges:
             part = pl.ds((lo + 1) * LANES, (hi - lo) * LANES)
-            for ways, source, target, distance in (
-                (level_up, up_out, below_in, 1),
-                (level_down, down_out, above_in, n_lev - 1),
+            for ways, source, target, distance, sent in (
+                (level_up, up_out, below_in, 1, lev_send.at[0]),
+                (level_down, down_out, above_in, n_lev - 1, lev_send.at[1]),
             ):
                 ways[stage].append(
                     pltpu.make_async_remote_copy(
                         src_ref=source.at[:, part],
                         dst_ref=target.at[:, part],
-                        send_sem=lev_send.at[index],
+                        send_sem=sent,
                         recv_sem=lev_recv.at[index],
                         device_id=(me, lax.rem(lev + distance, n_lev)),
                         device_id_type=MESH,
                     )
                 )
                 index += 1
+
+    def all_of(source, target, send_sem, recv_sem):
+        return pltpu.make_async_remote_copy(
+            src_ref=source,
+            dst_ref=target,
+            send_sem=send_sem,
+            recv_sem=recv_sem,
+            device_id=tile_at(1),
+            device_id_type=MESH,
+        )
+
+    seven = pl.ds(0, reach - 1)
+    all_forward = all_of(outgoing.at[seven], outgoing.at[seven], fwd_send, fwd_recv.at[0])
+    all_returns = all_of(back.at[seven], back.at[seven], fwd_send, fwd_recv.at[0])
+    all_halo = all_of(tiny_out, tiny_in, tiny_send, tiny_recv)
+    all_up = all_of(up_out, below_in, lev_send.at[0], lev_recv.at[0])
+    all_down = all_of(down_out, above_in, lev_send.at[1], lev_recv.at[0])
 
     def level_start(stage):
         @pl.when(lev < n_lev - 1)
@@ -533,7 +550,7 @@
         if lo == 0:
             adj[:, pl.ds(cols, span)] = value[:, :span]
 
-    for copy in (*halo_parts, *coef_edges):
+    for copy in (all_halo, *coef_edges):
         copy.wait_recv()
     finish_halo()
 
@@ -591,14 +608,7 @@
     level_wait(0)
     for lo, hi in early:
         tangent_finish(lo, hi)
-    for core in BOTH:
-
-        @pl.when(parity == core)
-        def _():
-            for name, copy in forward.items():
-                if core in plan[name][0]:
-                    copy.wait_send()
-
+    all_forward.wait_send()
     level_wait(1)
     for lo, hi in middle:
         tangent_finish(lo, hi)
@@ -644,20 +654,16 @@
         grads(groups)
         unslot(groups, again)
 
-    for copy in (*giving.values(), *coef_edges, *halo_parts):
+    for copy in (all_returns, all_halo, *coef_edges):
         copy.wait_send()
 
     @pl.when(lev < n_lev - 1)
     def _():
-        for copies in level_up:
-            for copy in copies:
-                copy.wait_send()
+        all_up.wait_send()
 
     @pl.when(lev > 0)
     def _():
-        for copies in level_down:
-            for copy in copies:
-                copy.wait_send()
+        all_down.wait_send()
 
 
 def store(tangent_ref, grad_ref, tangent_hbm, grad_hbm, sem):
@@ -717,13 +723,13 @@
             pltpu.VMEM((reach, cap // LANES + 3, rows, LANES), f32),
             dma((7,)),
             dma((len(FIRST),)),
-            dma((13,)),
+            dma,
             dma((14,)),
             dma((2,)),
             dma((2,)),
-            dma((4,)),
-            dma((4,)),
-            dma((8,)),
+            dma,
+            dma,
+            dma((2,)),
             dma((8,)),
             dma((reach,)),
         ],

time: 35.8 us -> 35.6 us (level)
  no operation moved by 1% of the time
where the time goes in v7:
time: 35.6 us; the launch traced here: 35.4 us
  Pallas kernels  34.8 us (98%)
  between operations  0.64 us (2%)
    pallas_call x1, Pallas kernels, shards(): pl.pallas_call(functools.partial(kernel, n_tile, n_lev), out_shape=(out,...  34 us
    pallas_call x1, Pallas kernels, shards(): pl.pallas_call(store, out_shape=(out, out), in_specs=(vmem, vmem), out_sp...  0.76 us

profile of v7, /device:TPU:1, one launch (start us, length us, event | category | flops | bytes accessed | tf_op | source)
XLA Modules:
  0.0 35.4 jit_solution(14732836720321286696)
XLA Ops:
  0.6 34.0 %shard_map.95 = (f32[3,8,2048]{2,1,0:T(8,128)S(1)}, f32[3,8,2048]{2,1,0:T(8,128)S(1)}) custom-call(bf16[3,8,2048]{2,1,0:T(8,128)(2,1)} %traj_hbm.1, bf16[3,8,2048]{2,1,0:T(8,128)(2,1)} %inc_hbm.1, s32[1,8]{1,0:T(1,128)} %counts_hbm.1, f32[3]{0:T(128)} %kappa_hbm.1, f32[1,2048]{1,0:T(1,128)} %bitcast.3, f32[1,2048]{1,0:T(1,128)} %bitcast.4, ...), custom_call_target="tpu_custom_call" | custom-call | tf_op jit(solution)/shard_map/pallas_call | solution.py:690
  34.7 0.8 %shard_map.96 = (f32[3,8,2048]{2,1,0:T(8,128)}, f32[3,8,2048]{2,1,0:T(8,128)}) custom-call(f32[3,8,2048]{2,1,0:T(8,128)S(1)} %get-tuple-element.4.tangent_ref, f32[3,8,2048]{2,1,0:T(8,128)S(1)} %get-tuple-element.5.grad_ref), custom_call_target="tpu_custom_call" | custom-call | tf_op jit(solution)/shard_map/pallas_call | solution.py:754
